TPU v7x, 32 devices: a whole 2x2x4 slice. The times are simulated.
32 devices in a mesh: row: 4 (over y, core), col: 8 (over z, x).
Axes of the slice: x: 2, y: 2, z: 4, core: 2. Of those that a mesh axis runs over, the one named last changes fastest.
Arguments:
- velocity_modes: bfloat16 [3, 176, 352, 704], P(None, 'row', 'col'), may hold values from -0.00090789795 to 0.00090789795
- wavenumbers: float32 [8], replicated, may hold values from 0.5 to 3
- polar: float32 [8], replicated, may hold values from -3.140625 to 3.140625
- azimuth: float32 [8], replicated, may hold values from -3.140625 to 3.140625
Outputs:
- velocity: bfloat16 [3, 512, 512, 512], P(None, 'row', 'col')
- far_field: float32 [8, 2, 8], P('col')
All inputs are finite; a program needn't handle non-finite values.
Results may differ from a plain program's by a relative error of at most 0.0075.
Values may be sent and summed in bfloat16 or wider, within the bound.
A program may use at most 192 MiB of HBM per device.

v0:
```python
import functools
import math

import jax
import jax.numpy as jnp
from jax import lax
from jax.experimental import pallas as pl
from jax.experimental.pallas import tpu as pltpu
from jax.sharding import PartitionSpec as P

VMEM_LIMIT = 60 * 1024 * 1024


def padded(count):
    return -(-count // 16) * 16


def angles(waves, points):
    cells = jnp.arange(points, dtype=jnp.int32)
    product = jnp.mod(waves[:, None] * cells[None, :], points)
    return product.astype(jnp.float32) * (2.0 * math.pi / points)


def z_table(modes, points, blocks):
    angle = angles(jnp.arange(modes, dtype=jnp.int32) - modes // 2, points)
    cosine = jnp.cos(angle).reshape(modes, blocks, 1, -1)
    sine = jnp.sin(angle).reshape(modes, blocks, 1, -1)
    table = jnp.concatenate(
        [jnp.concatenate([cosine, sine], 2), jnp.concatenate([-sine, cosine], 2)], 0
    )
    return table.reshape(2 * modes, 2 * points).astype(jnp.bfloat16)


def y_table(modes, points, sources, blocks):
    angle = angles(jnp.arange(modes, dtype=jnp.int32) - modes // 2, points).T
    both = jnp.stack([jnp.cos(angle), jnp.sin(angle)], 0)
    both = both.reshape(2, blocks, points // blocks, sources, modes // sources)
    extra = padded(modes // sources) - modes // sources
    both = jnp.pad(both, ((0, 0), (0, 0), (0, 0), (0, 0), (0, extra)))
    both = jnp.transpose(both, (1, 0, 2, 3, 4))
    return both.reshape(blocks, 2 * (points // blocks), -1).astype(jnp.bfloat16)


def x_table(count, points, sources):
    waves = jnp.arange(count, dtype=jnp.int32)
    angle = angles(waves, points)
    cosine = jnp.cos(angle).astype(jnp.bfloat16)
    sine = jnp.sin(angle).astype(jnp.bfloat16)
    factor = jnp.where(waves == 0, 1.0, 2.0).astype(jnp.bfloat16)[:, None]
    table = jnp.stack([factor * cosine, -(factor * sine)], 0)
    table = table.reshape(2, sources, count // sources, points)
    extra = padded(count // sources) - count // sources
    table = jnp.pad(table, ((0, 0), (0, 0), (0, extra), (0, 0)))
    return table.reshape(2, -1, points)


def estimate(rows, depth, columns):
    return pl.CostEstimate(
        flops=2 * rows * depth * columns,
        bytes_accessed=2 * (rows * depth + depth * columns + rows * columns),
        transcendentals=0,
    )


def along_z(modes_ref, table_ref, out_ref):
    slabs, ky = modes_ref.shape[1], modes_ref.shape[2]
    blocks, width = out_ref.shape[0], out_ref.shape[4]

    @pl.loop(0, slabs)
    def _(a):
        value = jnp.dot(modes_ref[0, a], table_ref[...], preferred_element_type=jnp.float32)
        value = value.astype(jnp.bfloat16)
        for block in range(blocks):
            out_ref[block, 0, a] = jnp.zeros(out_ref.shape[3:], jnp.bfloat16)
            out_ref[block, 0, a, 0:ky, :] = value[:, block * width : (block + 1) * width]


def along_y(moved_ref, table_ref, out_ref, total):
    slabs, width = moved_ref.shape[2], moved_ref.shape[4]
    half = width // 2
    rows = out_ref.shape[2]
    total[...] = jnp.zeros_like(total)
    group = 2 if slabs % 2 == 0 and width % 128 == 0 else 1
    for a in range(0, slabs, group):
        parts = [moved_ref[:, 0, a + g].reshape(-1, width) for g in range(group)]
        data = parts[0] if group == 1 else jnp.concatenate(parts, 1)
        product = jnp.dot(table_ref[0], data, preferred_element_type=jnp.float32)
        for g in range(group):
            by_cos = product[:rows, g * width : (g + 1) * width]
            by_sin = product[rows:, g * width : (g + 1) * width]
            turned = jnp.concatenate([-by_sin[:, half:], by_sin[:, :half]], 1)
            total[:, a + g, :] = by_cos + turned
    out_ref[0, 0] = total[...].astype(jnp.bfloat16)


def along_x(arrived_0, arrived_1, arrived_2, table_ref, phase_ref, weight_ref, cos_ref, sin_ref,
            velocity_ref, by_cos_ref, by_sin_ref, real_scr, imag_scr):
    ys, width = arrived_0.shape[2], arrived_0.shape[4]
    half = width // 2
    fields = []
    for c, arrived_ref in enumerate((arrived_0, arrived_1, arrived_2)):
        for y in range(ys):
            data = arrived_ref[:, 0, y].reshape(-1, width).T
            real_scr[c, y * half : (y + 1) * half, :] = data[:half]
            imag_scr[c, y * half : (y + 1) * half, :] = data[half:]
        field = jnp.dot(real_scr[c], table_ref[0], preferred_element_type=jnp.float32)
        field = field + jnp.dot(imag_scr[c], table_ref[1], preferred_element_type=jnp.float32)
        velocity_ref[c] = field.astype(jnp.bfloat16).reshape(velocity_ref.shape[1:])
        fields.append(field)
    f0, f1, f2 = fields
    trace = (f0 * f0 + f1 * f1 + f2 * f2) / 3.0
    stress = [f0 * f0 - trace, f1 * f1 - trace, f2 * f2 - trace, f0 * f1, f0 * f2, f1 * f2]
    mixed = None
    for index, part in enumerate(stress):
        line = jnp.dot(
            part.astype(jnp.bfloat16), phase_ref[...], preferred_element_type=jnp.float32
        )
        term = weight_ref[index : index + 1, :] * line
        mixed = term if mixed is None else mixed + term
    mixed = mixed.reshape(ys, half, -1)
    by_cos_ref[...] = jnp.sum(mixed * cos_ref[...][None], 1)
    by_sin_ref[...] = jnp.sum(mixed * sin_ref[...][None], 1)


def body(rows, cols, velocity_modes, wavenumbers, polar, azimuth):
    kx_local, ky_local, modes = velocity_modes.shape[1:]
    modes = modes // 2
    kx = kx_local * rows
    points = velocity_points(modes)
    y_local, z_local = points // rows, points // cols
    width = 2 * z_local
    ky_pad, kx_pad = padded(ky_local), padded(kx_local)

    table_z = z_table(modes, points, cols)
    table_y = y_table(modes, points, cols, rows)
    steps = 2 if kx_local % 2 == 0 else 1
    slabs = kx_local // steps
    arrived = []
    for c in range(3):
        first = pl.pallas_call(
            along_z,
            grid=(steps,),
            in_specs=[
                pl.BlockSpec((1, slabs, ky_local, 2 * modes), lambda i, c=c: (c, i, 0, 0)),
                pl.BlockSpec((2 * modes, 2 * points), lambda i: (0, 0)),
            ],
            out_specs=pl.BlockSpec((cols, 1, slabs, ky_pad, width), lambda i: (0, 0, i, 0, 0)),
            out_shape=jax.ShapeDtypeStruct((cols, 1, kx_local, ky_pad, width), jnp.bfloat16),
            compiler_params=pltpu.CompilerParams(vmem_limit_bytes=VMEM_LIMIT),
            cost_estimate=estimate(kx_local * ky_pad, 2 * modes, 2 * points),
            name=f"along_z_{c}",
        )(velocity_modes, table_z)
        moved = lax.all_to_all(first, "col", split_axis=0, concat_axis=0, tiled=True)
        second = pl.pallas_call(
            along_y,
            grid=(rows,),
            in_specs=[
                pl.BlockSpec((cols, 1, kx_local, ky_pad, width), lambda t: (0, 0, 0, 0, 0)),
                pl.BlockSpec((1, 2 * y_local, cols * ky_pad), lambda t: (t, 0, 0)),
            ],
            out_specs=pl.BlockSpec((1, 1, y_local, kx_pad, width), lambda t: (t, 0, 0, 0, 0)),
            out_shape=jax.ShapeDtypeStruct((rows, 1, y_local, kx_pad, width), jnp.bfloat16),
            scratch_shapes=[pltpu.VMEM((y_local, kx_pad, width), jnp.float32)],
            compiler_params=pltpu.CompilerParams(vmem_limit_bytes=VMEM_LIMIT),
            cost_estimate=estimate(2 * points, cols * ky_pad, kx_local * width),
            name=f"along_y_{c}",
        )(moved, table_y)
        arrived.append(lax.all_to_all(second, "row", split_axis=0, concat_axis=0, tiled=True))

    dirs, freqs = polar.shape[0], wavenumbers.shape[0]
    count = dirs * freqs
    wave_j = jnp.repeat(wavenumbers, dirs)
    axis_one = jnp.tile(jnp.sin(polar) * jnp.cos(azimuth), freqs)
    axis_two = jnp.tile(jnp.sin(polar) * jnp.sin(azimuth), freqs)
    axis_three = jnp.tile(jnp.cos(polar), freqs)
    unit = 2.0 * math.pi / points
    x_pos = jnp.arange(points, dtype=jnp.int32).astype(jnp.float32) * unit
    angle_x = wave_j[None, :] * (axis_one[None, :] * x_pos[:, None])
    phase_x = jnp.concatenate([jnp.cos(angle_x), -jnp.sin(angle_x)], 1).astype(jnp.bfloat16)
    weights = jnp.stack(
        [
            axis_one * axis_one,
            axis_two * axis_two,
            axis_three * axis_three,
            2.0 * axis_one * axis_two,
            2.0 * axis_one * axis_three,
            2.0 * axis_two * axis_three,
        ],
        0,
    )
    weights = jnp.concatenate([weights, weights], 1)
    z_index = lax.axis_index("col") * z_local + jnp.arange(z_local, dtype=jnp.int32)
    y_index = lax.axis_index("row") * y_local + jnp.arange(y_local, dtype=jnp.int32)
    angle_z = wave_j[None, :] * (axis_three[None, :] * (z_index.astype(jnp.float32) * unit)[:, None])
    angle_y = wave_j[None, :] * (axis_two[None, :] * (y_index.astype(jnp.float32) * unit)[:, None])
    cos_z, sin_z = jnp.cos(angle_z), jnp.sin(angle_z)

    ys = 8
    whole = lambda i: (0, 0)
    velocity, by_cos, by_sin = pl.pallas_call(
        along_x,
        grid=(y_local // ys,),
        in_specs=[
            *[pl.BlockSpec((rows, 1, ys, kx_pad, width), lambda i: (0, 0, i, 0, 0))] * 3,
            pl.BlockSpec((2, rows * kx_pad, points), lambda i: (0, 0, 0)),
            pl.BlockSpec((points, 2 * count), whole),
            pl.BlockSpec((6, 2 * count), whole),
            pl.BlockSpec((z_local, 2 * count), whole),
            pl.BlockSpec((z_local, 2 * count), whole),
        ],
        out_specs=[
            pl.BlockSpec((3, ys, z_local, points), lambda i: (0, i, 0, 0)),
            pl.BlockSpec((ys, 2 * count), lambda i: (i, 0)),
            pl.BlockSpec((ys, 2 * count), lambda i: (i, 0)),
        ],
        out_shape=[
            jax.ShapeDtypeStruct((3, y_local, z_local, points), jnp.bfloat16),
            jax.ShapeDtypeStruct((y_local, 2 * count), jnp.float32),
            jax.ShapeDtypeStruct((y_local, 2 * count), jnp.float32),
        ],
        scratch_shapes=[pltpu.VMEM((3, ys * z_local, rows * kx_pad), jnp.bfloat16)] * 2,
        compiler_params=pltpu.CompilerParams(vmem_limit_bytes=VMEM_LIMIT),
        name="along_x",
    )(
        *arrived,
        x_table(kx, points, rows),
        phase_x,
        weights,
        jnp.concatenate([cos_z, cos_z], 1),
        jnp.concatenate([sin_z, sin_z], 1),
    )
    real_part = by_cos[:, :count] + by_sin[:, count:]
    imag_part = by_cos[:, count:] - by_sin[:, :count]
    cos_y, sin_y = jnp.cos(angle_y), jnp.sin(angle_y)
    terms = jnp.stack(
        [
            jnp.sum(real_part * cos_y + imag_part * sin_y, 0),
            jnp.sum(imag_part * cos_y - real_part * sin_y, 0),
        ],
        0,
    )
    spectrum = terms.reshape(2, freqs, dirs) * (wavenumbers * wavenumbers)[None, :, None]
    spectrum = jnp.transpose(spectrum / points**1.5, (2, 0, 1))
    total = lax.psum(spectrum, ("row", "col"))
    owned = dirs // cols
    far_field = lax.dynamic_slice_in_dim(total, lax.axis_index("col") * owned, owned, 0)
    return (velocity, far_field)


def velocity_points(modes):
    return 1 << (modes - 1).bit_length()


def solution(mesh):
    return jax.shard_map(
        functools.partial(body, mesh.shape["row"], mesh.shape["col"]),
        mesh=mesh,
        in_specs=(P(None, "row", "col", None), P(), P(), P()),
        out_specs=(P(None, "row", "col", None), P("col", None, None)),
        check_vma=False,
    )
```

profile of v0, /device:TPU:0, one launch (start us, length us, event | category | flops | bytes accessed | tf_op | source)
XLA Modules:
  0.0 637.7 jit_solution(4326331050244163407)
XLA Ops:
  0.7 3.6 fusion.19
  4.9 1.6 copy.14.table_ref
  6.4 19.6 %along_z_2.1 = bf16[8,1,44,48,128]{4,3,2,1,0:T(8,128)(2,1)} custom-call(bf16[3,44,44,704]{3,2,1,0:T(8,128)(2,1)} %modes_ref.5, bf16[704,1024]{1,0:T(8,128)(2,1)} %copy.14.table_ref), custom_call_target="tpu_custom_call" | custom-call | flops 3045064704 | bytes 8740864 | tf_op jit(solution)/shard_map/along_z_2/pallas_call | solution.py:140
  26.0 7.3 %all-to-all-start.4 = ((bf16[8,1,44,48,128]{4,3,2,1,0:T(8,128)(2,1)}), bf16[8,1,44,48,128]{4,3,2,1,0:T(8,128)(2,1)}, u32[]{:S(2)}, u32[]{:S(2)}) async-start(bf16[8,1,44,48,128]{4,3,2,1,0:T(8,128)(2,1)} %along_z_2.1), calls=%async_computation.4 | async-start | bytes 8650752 | tf_op jit(solution)/shard_map/all_to_all | solution.py:153
  33.3 19.6 %along_z_1.1 = bf16[8,1,44,48,128]{4,3,2,1,0:T(8,128)(2,1)} custom-call(bf16[3,44,44,704]{3,2,1,0:T(8,128)(2,1)} %modes_ref.5, bf16[704,1024]{1,0:T(8,128)(2,1)} %copy.14.table_ref), custom_call_target="tpu_custom_call" | custom-call | flops 3045064704 | bytes 8740864 | tf_op jit(solution)/shard_map/along_z_1/pallas_call | solution.py:140
  52.9 76.5 %all-to-all-done.4.moved_ref = bf16[8,1,44,48,128]{4,3,2,1,0:T(8,128)(2,1)} async-done(((bf16[8,1,44,48,128]{4,3,2,1,0:T(8,128)(2,1)}), bf16[8,1,44,48,128]{4,3,2,1,0:T(8,128)(2,1)}, u32[]{:S(2)}, u32[]{:S(2)}) %all-to-all-start.4) | async-done | bytes 4325408 | tf_op jit(solution)/shard_map/all_to_all | solution.py:153
  129.4 4.6 all-to-all-start.2
  134.0 19.6 %along_z_0.1 = bf16[8,1,44,48,128]{4,3,2,1,0:T(8,128)(2,1)} custom-call(bf16[3,44,44,704]{3,2,1,0:T(8,128)(2,1)} %modes_ref.5, bf16[704,1024]{1,0:T(8,128)(2,1)} %copy.14.table_ref), custom_call_target="tpu_custom_call" | custom-call | flops 3045064704 | bytes 8740864 | tf_op jit(solution)/shard_map/along_z_0/pallas_call | solution.py:140
  153.6 75.7 %all-to-all-done.2.moved_ref = bf16[8,1,44,48,128]{4,3,2,1,0:T(8,128)(2,1)} async-done(((bf16[8,1,44,48,128]{4,3,2,1,0:T(8,128)(2,1)}), bf16[8,1,44,48,128]{4,3,2,1,0:T(8,128)(2,1)}, u32[]{:S(2)}, u32[]{:S(2)}) %all-to-all-start.2) | async-done | bytes 4325408 | tf_op jit(solution)/shard_map/all_to_all | solution.py:153
  229.3 4.6 all-to-all-start
  233.9 3.2 cosine_convert_fusion.1
  237.2 0.8 copy.15
  238.6 1.2 copy.16.table_ref
  239.7 14.8 %along_y_2.1 = bf16[4,1,128,48,128]{4,3,2,1,0:T(8,128)(2,1)} custom-call(bf16[8,1,44,48,128]{4,3,2,1,0:T(8,128)(2,1)} %all-to-all-done.4.moved_ref, bf16[4,256,384]{2,1,0:T(8,128)(2,1)} %copy.16.table_ref), custom_call_target="tpu_custom_call" | custom-call | flops 4429185024 | bytes 16646144 | tf_op jit(solution)/shard_map/along_y_2/pallas_call | solution.py:154
  254.5 74.7 %all-to-all-done.moved_ref = bf16[8,1,44,48,128]{4,3,2,1,0:T(8,128)(2,1)} async-done(((bf16[8,1,44,48,128]{4,3,2,1,0:T(8,128)(2,1)}), bf16[8,1,44,48,128]{4,3,2,1,0:T(8,128)(2,1)}, u32[]{:S(2)}, u32[]{:S(2)}) %all-to-all-start) | async-done | bytes 4325408 | tf_op jit(solution)/shard_map/all_to_all | solution.py:153
  329.2 5.3 all-to-all-start.5
  334.5 14.8 %along_y_1.1 = bf16[4,1,128,48,128]{4,3,2,1,0:T(8,128)(2,1)} custom-call(bf16[8,1,44,48,128]{4,3,2,1,0:T(8,128)(2,1)} %all-to-all-done.2.moved_ref, bf16[4,256,384]{2,1,0:T(8,128)(2,1)} %copy.16.table_ref), custom_call_target="tpu_custom_call" | custom-call | flops 4429185024 | bytes 16646144 | tf_op jit(solution)/shard_map/along_y_1/pallas_call | solution.py:154
  349.3 55.8 %all-to-all-done.5.arrived_2 = bf16[4,1,128,48,128]{4,3,2,1,0:T(8,128)(2,1)} async-done(((bf16[4,1,128,48,128]{4,3,2,1,0:T(8,128)(2,1)}), bf16[4,1,128,48,128]{4,3,2,1,0:T(8,128)(2,1)}, u32[]{:S(2)}, u32[]{:S(2)}) %all-to-all-start.5) | async-done | bytes 6291488 | tf_op jit(solution)/shard_map/all_to_all | solution.py:168
  405.2 5.4 all-to-all-start.3
  410.6 14.8 %along_y_0.1 = bf16[4,1,128,48,128]{4,3,2,1,0:T(8,128)(2,1)} custom-call(bf16[8,1,44,48,128]{4,3,2,1,0:T(8,128)(2,1)} %all-to-all-done.moved_ref, bf16[4,256,384]{2,1,0:T(8,128)(2,1)} %copy.16.table_ref), custom_call_target="tpu_custom_call" | custom-call | flops 4429185024 | bytes 16646144 | tf_op jit(solution)/shard_map/along_y_0/pallas_call | solution.py:154
  425.4 55.7 %all-to-all-done.3.arrived_1 = bf16[4,1,128,48,128]{4,3,2,1,0:T(8,128)(2,1)} async-done(((bf16[4,1,128,48,128]{4,3,2,1,0:T(8,128)(2,1)}), bf16[4,1,128,48,128]{4,3,2,1,0:T(8,128)(2,1)}, u32[]{:S(2)}, u32[]{:S(2)}) %all-to-all-start.3) | async-done | bytes 6291488 | tf_op jit(solution)/shard_map/all_to_all | solution.py:168
  481.1 5.3 all-to-all-start.1
  487.3 0.7 pad_maximum_fusion.3.weight_ref
  488.2 0.7 pad_maximum_fusion.1
  488.9 1.1 cosine_convert_fusion.3
  490.1 0.8 pad_maximum_fusion.phase_ref
  490.8 1.9 fusion.21
  492.7 0.8 fusion.15
  493.5 63.5 %all-to-all-done.1.arrived_0 = bf16[4,1,128,48,128]{4,3,2,1,0:T(8,128)(2,1)} async-done(((bf16[4,1,128,48,128]{4,3,2,1,0:T(8,128)(2,1)}), bf16[4,1,128,48,128]{4,3,2,1,0:T(8,128)(2,1)}, u32[]{:S(2)}, u32[]{:S(2)}) %all-to-all-start.1) | async-done | bytes 6291488 | tf_op jit(solution)/shard_map/all_to_all | solution.py:168
  557.0 40.9 %along_x.1 = (bf16[3,128,64,512]{3,2,1,0:T(8,128)(2,1)}, f32[128,128]{1,0:T(8,128)}, f32[128,128]{1,0:T(8,128)}) custom-call(bf16[4,1,128,48,128]{4,3,2,1,0:T(8,128)(2,1)} %all-to-all-done.1.arrived_0, bf16[4,1,128,48,128]{4,3,2,1,0:T(8,128)(2,1)} %all-to-all-done.3.arrived_1, bf16[4,1,128,48,128]{4,3,2,1,0:T(8,128)(2,1)} %all-to-all-done.5.arrived_2, ...), custom_call_target="tpu_custom_call" | custom-call | tf_op jit(solution)/shard_map/along_x/pallas_call | solution.py:200
  597.9 1.3 add_reduce_fusion
  599.4 37.6 %psum.7 = f32[8,2,8]{0,2,1:T(8,128)S(1)} all-reduce(f32[8,2,8]{0,2,1:T(8,128)S(1)} %fusion.29), channel_id=1, replica_groups=mesh['row'=4,'col'=8] {'row','col'}, use_global_device_ids=true, to_apply=%region_2.3 | all-reduce | flops 128 | bytes 1024 | tf_op jit(solution)/shard_map/psum | solution.py:244
  (44 shorter events, 3.2 us)
Async XLA Ops:
  26.0 103.4 %all-to-all-start.4 = ((bf16[8,1,44,48,128]{4,3,2,1,0:T(8,128)(2,1)}), bf16[8,1,44,48,128]{4,3,2,1,0:T(8,128)(2,1)}, u32[]{:S(2)}, u32[]{:S(2)}) async-start(bf16[8,1,44,48,128]{4,3,2,1,0:T(8,128)(2,1)} %along_z_2.1), calls=%async_computation.4 | async-start | bytes 8650752 | tf_op jit(solution)/shard_map/all_to_all | solution.py:153
  129.4 99.9 %all-to-all-start.2 = ((bf16[8,1,44,48,128]{4,3,2,1,0:T(8,128)(2,1)}), bf16[8,1,44,48,128]{4,3,2,1,0:T(8,128)(2,1)}, u32[]{:S(2)}, u32[]{:S(2)}) async-start(bf16[8,1,44,48,128]{4,3,2,1,0:T(8,128)(2,1)} %along_z_1.1), calls=%async_computation.2 | async-start | bytes 8650752 | tf_op jit(solution)/shard_map/all_to_all | solution.py:153
  229.3 99.9 %all-to-all-start = ((bf16[8,1,44,48,128]{4,3,2,1,0:T(8,128)(2,1)}), bf16[8,1,44,48,128]{4,3,2,1,0:T(8,128)(2,1)}, u32[]{:S(2)}, u32[]{:S(2)}) async-start(bf16[8,1,44,48,128]{4,3,2,1,0:T(8,128)(2,1)} %along_z_0.1), calls=%async_computation | async-start | bytes 8650752 | tf_op jit(solution)/shard_map/all_to_all | solution.py:153
  329.2 75.9 %all-to-all-start.5 = ((bf16[4,1,128,48,128]{4,3,2,1,0:T(8,128)(2,1)}), bf16[4,1,128,48,128]{4,3,2,1,0:T(8,128)(2,1)}, u32[]{:S(2)}, u32[]{:S(2)}) async-start(bf16[4,1,128,48,128]{4,3,2,1,0:T(8,128)(2,1)} %along_y_2.1), calls=%async_computation.5 | async-start | bytes 12582912 | tf_op jit(solution)/shard_map/all_to_all | solution.py:168
  405.2 75.9 %all-to-all-start.3 = ((bf16[4,1,128,48,128]{4,3,2,1,0:T(8,128)(2,1)}), bf16[4,1,128,48,128]{4,3,2,1,0:T(8,128)(2,1)}, u32[]{:S(2)}, u32[]{:S(2)}) async-start(bf16[4,1,128,48,128]{4,3,2,1,0:T(8,128)(2,1)} %along_y_1.1), calls=%async_computation.3 | async-start | bytes 12582912 | tf_op jit(solution)/shard_map/all_to_all | solution.py:168
  425.4 61.0 %copy-start.2 = (f32[8]{0:T(128)S(1)}, f32[8]{0:T(128)}, u32[]{:S(2)}) copy-start(f32[8]{0:T(128)} %param.6) | copy-start | bytes 100
  425.4 61.2 %copy-start = (f32[8]{0:T(128)S(1)}, f32[8]{0:T(128)}, u32[]{:S(2)}) copy-start(f32[8]{0:T(128)} %param.7) | copy-start | bytes 100
  425.4 61.4 %copy-start.1 = (f32[8]{0:T(128)S(1)}, f32[8]{0:T(128)}, u32[]{:S(2)}) copy-start(f32[8]{0:T(128)} %param.5) | copy-start | bytes 100
  481.1 75.9 %all-to-all-start.1 = ((bf16[4,1,128,48,128]{4,3,2,1,0:T(8,128)(2,1)}), bf16[4,1,128,48,128]{4,3,2,1,0:T(8,128)(2,1)}, u32[]{:S(2)}, u32[]{:S(2)}) async-start(bf16[4,1,128,48,128]{4,3,2,1,0:T(8,128)(2,1)} %along_y_0.1), calls=%async_computation.1 | async-start | bytes 12582912 | tf_op jit(solution)/shard_map/all_to_all | solution.py:168
where the time goes:
time: 638 us
  waiting for transfers between devices  402 us (63%)
  Pallas kernels  144 us (23%)
  blocking collectives  37.6 us (6%)
  starting transfers between devices  32.4 us (5%)
  other arithmetic  15.1 us (2%)
    all_to_all x3, waiting for transfers between devices, body(): lax.all_to_all(first, 'col', split_axis=0, concat_axis=0, tiled=True)  227 us
    all_to_all x3, waiting for transfers between devices, body(): lax.all_to_all(second, 'row', split_axis=0, concat_axis=0, tiled=True)  175 us
    pallas_call x3, Pallas kernels, body(): pl.pallas_call(along_z, grid=(steps,), in_specs=[pl.BlockSpec((1, slabs,...  58.8 us
    pallas_call x3, Pallas kernels, body(): pl.pallas_call(along_y, grid=(rows,), in_specs=[pl.BlockSpec((cols, 1, kx...  44.4 us
    pallas_call x1, Pallas kernels, body(): pl.pallas_call(along_x, grid=(y_local // ys,), in_specs=[*[pl.BlockSpec((...  40.9 us
    psum x1, blocking collectives, body(): total = lax.psum(spectrum, ('row', 'col'))  37.6 us
    all_to_all x3, starting transfers between devices, body(): lax.all_to_all(first, 'col', split_axis=0, concat_axis=0, tiled=True)  16.4 us
    all_to_all x3, starting transfers between devices, body(): lax.all_to_all(second, 'row', split_axis=0, concat_axis=0, tiled=True)  15.9 us
  transfers between devices with their start and end apart: 6, of which 6 were waited for; matrix products, arithmetic and copies ran while one was open for 2% of the time, Pallas kernels for 13%

commit v1 on v0

--- a/solution.py
+++ b/solution.py
@@ -15,14 +15,21 @@
     return -(-count // 16) * 16
 
 
-def angles(waves, points):
-    cells = jnp.arange(points, dtype=jnp.int32)
+def phases(waves, cells, points):
     product = jnp.mod(waves[:, None] * cells[None, :], points)
     return product.astype(jnp.float32) * (2.0 * math.pi / points)
 
 
+def turned(count, axis, step):
+    return jnp.mod(lax.axis_index(axis) + step * jnp.arange(count, dtype=jnp.int32), count)
+
+
 def z_table(modes, points, blocks):
-    angle = angles(jnp.arange(modes, dtype=jnp.int32) - modes // 2, points)
+    cells = points // blocks
+    owner = turned(blocks, "col", 1)
+    at = (owner[:, None] * cells + jnp.arange(cells, dtype=jnp.int32)[None, :]).reshape(-1)
+    waves = jnp.arange(modes, dtype=jnp.int32) - modes // 2
+    angle = phases(waves, at, points)
     cosine = jnp.cos(angle).reshape(modes, blocks, 1, -1)
     sine = jnp.sin(angle).reshape(modes, blocks, 1, -1)
     table = jnp.concatenate(
@@ -32,26 +39,30 @@
 
 
 def y_table(modes, points, sources, blocks):
-    angle = angles(jnp.arange(modes, dtype=jnp.int32) - modes // 2, points).T
-    both = jnp.stack([jnp.cos(angle), jnp.sin(angle)], 0)
-    both = both.reshape(2, blocks, points // blocks, sources, modes // sources)
-    extra = padded(modes // sources) - modes // sources
-    both = jnp.pad(both, ((0, 0), (0, 0), (0, 0), (0, 0), (0, extra)))
-    both = jnp.transpose(both, (1, 0, 2, 3, 4))
-    return both.reshape(blocks, 2 * (points // blocks), -1).astype(jnp.bfloat16)
+    cells, held = points // blocks, modes // sources
+    extra = padded(held)
+    owner = turned(blocks, "row", 1)
+    at = owner[:, None] * cells + jnp.arange(cells, dtype=jnp.int32)[None, :]
+    slot = jnp.arange(extra, dtype=jnp.int32)
+    waves = turned(sources, "col", -1)[:, None] * held + slot[None, :] - modes // 2
+    angle = phases(at.reshape(-1), waves.reshape(-1), points)
+    keep = jnp.tile(slot < held, sources)[None, :]
+    both = jnp.stack([jnp.where(keep, jnp.cos(angle), 0.0), jnp.where(keep, jnp.sin(angle), 0.0)], 0)
+    both = both.reshape(2, blocks, cells, -1)
+    return jnp.transpose(both, (1, 0, 2, 3)).reshape(blocks, 2 * cells, -1).astype(jnp.bfloat16)
 
 
 def x_table(count, points, sources):
-    waves = jnp.arange(count, dtype=jnp.int32)
-    angle = angles(waves, points)
+    held = count // sources
+    extra = padded(held)
+    slot = jnp.arange(extra, dtype=jnp.int32)
+    waves = (turned(sources, "row", -1)[:, None] * held + slot[None, :]).reshape(-1)
+    keep = jnp.tile(slot < held, sources)
+    angle = phases(waves, jnp.arange(points, dtype=jnp.int32), points)
     cosine = jnp.cos(angle).astype(jnp.bfloat16)
     sine = jnp.sin(angle).astype(jnp.bfloat16)
-    factor = jnp.where(waves == 0, 1.0, 2.0).astype(jnp.bfloat16)[:, None]
-    table = jnp.stack([factor * cosine, -(factor * sine)], 0)
-    table = table.reshape(2, sources, count // sources, points)
-    extra = padded(count // sources) - count // sources
-    table = jnp.pad(table, ((0, 0), (0, 0), (0, extra), (0, 0)))
-    return table.reshape(2, -1, points)
+    factor = jnp.where(keep, jnp.where(waves == 0, 1.0, 2.0), 0.0).astype(jnp.bfloat16)[:, None]
+    return jnp.stack([factor * cosine, -(factor * sine)], 0)
 
 
 def estimate(rows, depth, columns):
@@ -62,35 +73,119 @@
     )
 
 
-def along_z(modes_ref, table_ref, out_ref):
-    slabs, ky = modes_ref.shape[1], modes_ref.shape[2]
-    blocks, width = out_ref.shape[0], out_ref.shape[4]
-
-    @pl.loop(0, slabs)
-    def _(a):
-        value = jnp.dot(modes_ref[0, a], table_ref[...], preferred_element_type=jnp.float32)
-        value = value.astype(jnp.bfloat16)
-        for block in range(blocks):
-            out_ref[block, 0, a] = jnp.zeros(out_ref.shape[3:], jnp.bfloat16)
-            out_ref[block, 0, a, 0:ky, :] = value[:, block * width : (block + 1) * width]
-
-
-def along_y(moved_ref, table_ref, out_ref, total):
-    slabs, width = moved_ref.shape[2], moved_ref.shape[4]
+MESH = pl.DeviceIdType.MESH
+CHUNK = 16
+
+
+def exchange(rows, cols, modes_ref, table_z, table_y, out_ref, modes, sent, came, total, passed,
+             in_sem, send_z, recv_z, send_y, recv_y):
+    kx, ky = modes.shape[1], modes.shape[2]
+    ky_pad, width = came.shape[3], came.shape[4]
     half = width // 2
-    rows = out_ref.shape[2]
+    y_local = out_ref.shape[2]
+    at_col, at_row = lax.axis_index("col"), lax.axis_index("row")
+    pieces = [(start, min(CHUNK, kx - start)) for start in range(0, kx, CHUNK)]
+    count = len(pieces)
+    col_peer = [lax.rem(at_col + r, cols) for r in range(cols)]
+    row_peer = [lax.rem(at_row + r, rows) for r in range(rows)]
+
+    def load(c):
+        return pltpu.make_async_copy(modes_ref.at[c], modes.at[c], in_sem.at[c])
+
+    for c in range(3):
+        load(c).start()
+    barrier = pltpu.get_barrier_semaphore()
+    for r in range(1, cols):
+        pl.semaphore_signal(barrier, inc=1, device_id={"col": col_peer[r]}, device_id_type=MESH)
+    for r in range(1, rows):
+        pl.semaphore_signal(barrier, inc=1, device_id={"row": row_peer[r]}, device_id_type=MESH)
+
+    def z_copy(t, r, size):
+        return pltpu.make_async_remote_copy(
+            src_ref=sent.at[t, r - 1, pl.ds(0, size)], dst_ref=came.at[t, r, pl.ds(0, size)],
+            send_sem=send_z.at[t, r], recv_sem=recv_z.at[t, r],
+            device_id={"col": col_peer[r]}, device_id_type=MESH)
+
+    def y_copy(c, j, r):
+        return pltpu.make_async_remote_copy(
+            src_ref=passed.at[j, r], dst_ref=out_ref.at[r, c, :, pl.ds(j * CHUNK, CHUNK), :],
+            send_sem=send_y.at[c, j, r], recv_sem=recv_y.at[c, j, r],
+            device_id={"row": row_peer[r]}, device_id_type=MESH)
+
+    def y_own(c, j):
+        return pltpu.make_async_copy(
+            passed.at[j, 0], out_ref.at[0, c, :, pl.ds(j * CHUNK, CHUNK), :], send_y.at[c, j, 0])
+
     total[...] = jnp.zeros_like(total)
-    group = 2 if slabs % 2 == 0 and width % 128 == 0 else 1
-    for a in range(0, slabs, group):
-        parts = [moved_ref[:, 0, a + g].reshape(-1, width) for g in range(group)]
-        data = parts[0] if group == 1 else jnp.concatenate(parts, 1)
-        product = jnp.dot(table_ref[0], data, preferred_element_type=jnp.float32)
-        for g in range(group):
-            by_cos = product[:rows, g * width : (g + 1) * width]
-            by_sin = product[rows:, g * width : (g + 1) * width]
-            turned = jnp.concatenate([-by_sin[:, half:], by_sin[:, :half]], 1)
-            total[:, a + g, :] = by_cos + turned
-    out_ref[0, 0] = total[...].astype(jnp.bfloat16)
+
+    @pl.loop(0, 3)
+    def _(c):
+        load(c).wait()
+        for j, (start, size) in enumerate(pieces):
+            t = c * count + j
+
+            @pl.loop(0, size)
+            def _(a):
+                value = jnp.dot(modes[c, start + a], table_z[...], preferred_element_type=jnp.float32)
+                value = value.astype(jnp.bfloat16)
+                for r in range(cols):
+                    to = came.at[t, 0, a] if r == 0 else sent.at[t, r - 1, a]
+                    to[...] = jnp.zeros(to.shape, jnp.bfloat16)
+                    to[0:ky, :] = value[:, r * width : (r + 1) * width]
+
+            if j == 0:
+                @pl.when(c == 0)
+                def _():
+                    pl.semaphore_wait(barrier, cols + rows - 2)
+            for r in range(1, cols):
+                z_copy(t, r, size).start()
+
+    @pl.loop(0, 3)
+    def _(c):
+        for j, (start, size) in enumerate(pieces):
+            t = c * count + j
+            for r in range(1, cols):
+                z_copy(t, r, size).wait_recv()
+
+            @pl.when(c > 0)
+            def _():
+                y_own(c - 1, j).wait()
+                for r in range(1, rows):
+                    y_copy(c - 1, j, r).wait_send()
+
+            group = 2 if size % 2 == 0 and width % 128 == 0 else 1
+
+            @pl.loop(0, rows)
+            def _(b):
+                for a in range(0, size, group):
+                    parts = [came[t, :, a + g].reshape(-1, width) for g in range(group)]
+                    data = parts[0] if group == 1 else jnp.concatenate(parts, 1)
+                    product = jnp.dot(table_y[b], data, preferred_element_type=jnp.float32)
+                    for g in range(group):
+                        by_cos = product[:y_local, g * width : (g + 1) * width]
+                        by_sin = product[y_local:, g * width : (g + 1) * width]
+                        swap = jnp.concatenate([-by_sin[:, half:], by_sin[:, :half]], 1)
+                        total[:, a + g, :] = by_cos + swap
+                if size < CHUNK:
+                    total[:, size:, :] = jnp.zeros((y_local, CHUNK - size, width), jnp.float32)
+                passed[j, b] = total[...].astype(jnp.bfloat16)
+
+            y_own(c, j).start()
+            for r in range(1, rows):
+                y_copy(c, j, r).start()
+
+    @pl.loop(0, 3)
+    def _(c):
+        for j, (start, size) in enumerate(pieces):
+            for r in range(1, cols):
+                z_copy(c * count + j, r, size).wait_send()
+            for r in range(1, rows):
+                y_copy(c, j, r).wait_recv()
+
+    for j in range(count):
+        y_own(2, j).wait()
+        for r in range(1, rows):
+            y_copy(2, j, r).wait_send()
 
 
 def along_x(arrived_0, arrived_1, arrived_2, table_ref, phase_ref, weight_ref, cos_ref, sin_ref,
@@ -133,39 +228,34 @@
 
     table_z = z_table(modes, points, cols)
     table_y = y_table(modes, points, cols, rows)
-    steps = 2 if kx_local % 2 == 0 else 1
-    slabs = kx_local // steps
-    arrived = []
-    for c in range(3):
-        first = pl.pallas_call(
-            along_z,
-            grid=(steps,),
-            in_specs=[
-                pl.BlockSpec((1, slabs, ky_local, 2 * modes), lambda i, c=c: (c, i, 0, 0)),
-                pl.BlockSpec((2 * modes, 2 * points), lambda i: (0, 0)),
-            ],
-            out_specs=pl.BlockSpec((cols, 1, slabs, ky_pad, width), lambda i: (0, 0, i, 0, 0)),
-            out_shape=jax.ShapeDtypeStruct((cols, 1, kx_local, ky_pad, width), jnp.bfloat16),
-            compiler_params=pltpu.CompilerParams(vmem_limit_bytes=VMEM_LIMIT),
-            cost_estimate=estimate(kx_local * ky_pad, 2 * modes, 2 * points),
-            name=f"along_z_{c}",
-        )(velocity_modes, table_z)
-        moved = lax.all_to_all(first, "col", split_axis=0, concat_axis=0, tiled=True)
-        second = pl.pallas_call(
-            along_y,
-            grid=(rows,),
-            in_specs=[
-                pl.BlockSpec((cols, 1, kx_local, ky_pad, width), lambda t: (0, 0, 0, 0, 0)),
-                pl.BlockSpec((1, 2 * y_local, cols * ky_pad), lambda t: (t, 0, 0)),
-            ],
-            out_specs=pl.BlockSpec((1, 1, y_local, kx_pad, width), lambda t: (t, 0, 0, 0, 0)),
-            out_shape=jax.ShapeDtypeStruct((rows, 1, y_local, kx_pad, width), jnp.bfloat16),
-            scratch_shapes=[pltpu.VMEM((y_local, kx_pad, width), jnp.float32)],
-            compiler_params=pltpu.CompilerParams(vmem_limit_bytes=VMEM_LIMIT),
-            cost_estimate=estimate(2 * points, cols * ky_pad, kx_local * width),
-            name=f"along_y_{c}",
-        )(moved, table_y)
-        arrived.append(lax.all_to_all(second, "row", split_axis=0, concat_axis=0, tiled=True))
+    count_t = 3 * (kx_pad // CHUNK)
+    arrived = pl.pallas_call(
+        functools.partial(exchange, rows, cols),
+        in_specs=[
+            pl.BlockSpec(memory_space=pl.ANY),
+            pl.BlockSpec(memory_space=pltpu.VMEM),
+            pl.BlockSpec(memory_space=pltpu.VMEM),
+        ],
+        out_specs=pl.BlockSpec(memory_space=pl.ANY),
+        out_shape=jax.ShapeDtypeStruct((rows, 3, y_local, kx_pad, width), jnp.bfloat16),
+        scratch_shapes=[
+            pltpu.VMEM(velocity_modes.shape, jnp.bfloat16),
+            pltpu.VMEM((count_t, cols - 1, CHUNK, ky_pad, width), jnp.bfloat16),
+            pltpu.VMEM((count_t, cols, CHUNK, ky_pad, width), jnp.bfloat16),
+            pltpu.VMEM((y_local, CHUNK, width), jnp.float32),
+            pltpu.VMEM((kx_pad // CHUNK, rows, y_local, CHUNK, width), jnp.bfloat16),
+            pltpu.SemaphoreType.DMA((3,)),
+            pltpu.SemaphoreType.DMA((count_t, cols)),
+            pltpu.SemaphoreType.DMA((count_t, cols)),
+            pltpu.SemaphoreType.DMA((3, kx_pad // CHUNK, rows)),
+            pltpu.SemaphoreType.DMA((3, kx_pad // CHUNK, rows)),
+        ],
+        compiler_params=pltpu.CompilerParams(
+            vmem_limit_bytes=VMEM_LIMIT, collective_id=0, has_side_effects=True
+        ),
+        cost_estimate=estimate(3 * 2 * points, cols * ky_pad, 2 * kx_local * width),
+        name="exchange",
+    )(velocity_modes, table_z, table_y)
 
     dirs, freqs = polar.shape[0], wavenumbers.shape[0]
     count = dirs * freqs
@@ -201,7 +291,10 @@
         along_x,
         grid=(y_local // ys,),
         in_specs=[
-            *[pl.BlockSpec((rows, 1, ys, kx_pad, width), lambda i: (0, 0, i, 0, 0))] * 3,
+            *[
+                pl.BlockSpec((rows, 1, ys, kx_pad, width), lambda i, c=c: (0, c, i, 0, 0))
+                for c in range(3)
+            ],
             pl.BlockSpec((2, rows * kx_pad, points), lambda i: (0, 0, 0)),
             pl.BlockSpec((points, 2 * count), whole),
             pl.BlockSpec((6, 2 * count), whole),
@@ -222,7 +315,9 @@
         compiler_params=pltpu.CompilerParams(vmem_limit_bytes=VMEM_LIMIT),
         name="along_x",
     )(
-        *arrived,
+        arrived,
+        arrived,
+        arrived,
         x_table(kx, points, rows),
         phase_x,
         weights,

time: 638 us -> 457 us (0.72)
  waiting for transfers between devices: 402 us -> 0 us
  Pallas kernels: 144 us -> 381 us
  starting transfers between devices: 32.4 us -> 0 us
  blocking collectives: 37.6 us -> 51.4 us
    all_to_all x6 -> x0, waiting for transfers between devices: 402 us -> none  [the longest x3 227 us: body(): lax.all_to_all(first, 'col', split_axis=0, concat_axis=0, tiled=True)]
    pallas_call x6 -> x1, Pallas kernels: 103 us -> 340 us  [body(): pl.pallas_call(functools.partial(exchange, rows, cols), in_specs=[pl.Bloc...]
    all_to_all x6 -> x0, starting transfers between devices: 32.4 us -> none  [the longest x3 16.4 us: body(): lax.all_to_all(first, 'col', split_axis=0, concat_axis=0, tiled=True)]
    psum x1, blocking collectives: 37.6 us -> 51.4 us  [body(): total = lax.psum(spectrum, ('row', 'col'))]
  transfers between devices with their start and end apart: 6 -> 0, of which waited for: 6 -> 0; matrix products, arithmetic and copies ran while one was open for 2% -> 0% of each run, Pallas kernels for 13% -> 0%
where the time goes in v1:
time: 457 us; the launch traced here: 456 us
  Pallas kernels  381 us (83%)
  blocking collectives  51.4 us (11%)
  other arithmetic  18.1 us (4%)
  local copies, waits for them, and re-layouts  4.86 us (1%)
    pallas_call x1, Pallas kernels, body(): pl.pallas_call(functools.partial(exchange, rows, cols), in_specs=[pl.Bloc...  340 us
    psum x1, blocking collectives, body(): total = lax.psum(spectrum, ('row', 'col'))  51.4 us
    pallas_call x1, Pallas kernels, body(): pl.pallas_call(along_x, grid=(y_local // ys,), in_specs=[*[pl.BlockSpec((...  41 us

profile of v1, /device:TPU:0, one launch (start us, length us, event | category | flops | bytes accessed | tf_op | source)
XLA Modules:
  0.0 456.4 jit_solution(11999760336111539569)
XLA Ops:
  0.7 0.1 tile.48
  0.8 0.1 broadcast_in_dim.52
  0.9 0.7 mul.507
  1.6 0.7 fusion.33
  2.4 0.7 broadcast_multiply_fusion
  3.2 0.1 add.272
  3.3 0.1 mul.486
  3.5 0.1 mul.467
  3.6 0.1 mul.475
  3.6 0.1 mul.480
  3.8 0.1 mul.495
  3.9 0.1 tile.52
  4.0 0.7 pad_maximum_fusion.5.weight_ref
  4.7 0.1 sub.18
  4.8 0.7 broadcast_in_dim.58
  5.6 0.1 mul.464
  5.6 0.2 fusion.19
  5.8 0.7 pad_maximum_fusion.3
  6.6 1.1 cosine_convert_fusion.2
  7.7 0.8 pad_maximum_fusion.2.phase_ref
  8.5 1.9 fusion.14
  10.4 0.8 pad_maximum_fusion.1.table_ref
  11.2 3.6 select_convert_fusion.1
  14.7 1.0 pad_maximum_fusion
  15.7 3.5 fusion.12
  19.3 0.6 maximum_maximum_fusion
  19.9 1.5 copy.9.table_z
  21.4 340.3 %exchange.1.arrived_0.arrived_1.arrived_2 = bf16[4,3,128,48,128]{4,3,2,1,0:T(8,128)(2,1)} custom-call(bf16[3,44,44,704]{3,2,1,0:T(8,128)(2,1)} %modes_ref.1, bf16[704,1024]{1,0:T(8,128)(2,1)} %copy.9.table_z, bf16[4,256,384]{2,1,0:T(8,128)(2,1)} %bitcast.7), custom_call_target="tpu_custom_call" | custom-call | flops 26575110144 | bytes 80216064 | tf_op jit(solution)/shard_map/exchange/pallas_call | solution.py:232
  361.8 41.0 %along_x.1 = (bf16[3,128,64,512]{3,2,1,0:T(8,128)(2,1)}, f32[128,128]{1,0:T(8,128)}, f32[128,128]{1,0:T(8,128)}) custom-call(bf16[4,3,128,48,128]{4,3,2,1,0:T(8,128)(2,1)} %exchange.1.arrived_0.arrived_1.arrived_2, bf16[4,3,128,48,128]{4,3,2,1,0:T(8,128)(2,1)} %exchange.1.arrived_0.arrived_1.arrived_2, ...), custom_call_target="tpu_custom_call" | custom-call | tf_op jit(solution)/shard_map/along_x/pallas_call | solution.py:290
  402.8 1.3 add_reduce_fusion
  404.3 51.4 %psum.7 = f32[8,2,8]{0,2,1:T(8,128)S(1)} all-reduce(f32[8,2,8]{0,2,1:T(8,128)S(1)} %fusion.22), channel_id=1, replica_groups=mesh['row'=4,'col'=8] {'row','col'}, use_global_device_ids=true, to_apply=%region_2.3 | all-reduce | flops 128 | bytes 1024 | tf_op jit(solution)/shard_map/psum | solution.py:339
  455.8 0.6 copy.11
  (27 shorter events, 0.8 us)

commit v2 on v1

v2 whole, which is shorter than its diff:
```python
import functools
import math

import jax
import jax.numpy as jnp
import numpy as np
from jax import lax
from jax.experimental import pallas as pl
from jax.experimental.pallas import tpu as pltpu
from jax.sharding import PartitionSpec as P

VMEM_LIMIT = 60 * 1024 * 1024


def padded(count):
    return -(-count // 16) * 16


def circle(waves, cells, points):
    angle = np.mod(np.outer(waves, cells), points).astype(np.float64) * (2.0 * math.pi / points)
    return np.cos(angle).astype(np.float32), np.sin(angle).astype(np.float32)


def z_table(modes, points, blocks):
    cosine, sine = circle(np.arange(modes) - modes // 2, np.arange(points), points)
    cosine, sine = (part.reshape(modes, blocks, 1, -1) for part in (cosine, sine))
    table = np.concatenate(
        [np.concatenate([cosine, sine], 2), np.concatenate([-sine, cosine], 2)], 0
    )
    return jnp.asarray(table.reshape(2 * modes, 2 * points).astype(jnp.bfloat16))


def y_table(modes, points, sources, blocks, held_rows):
    cosine, sine = circle(np.arange(points), np.arange(modes) - modes // 2, points)
    both = np.stack([cosine, sine], 0)
    both = both.reshape(2, blocks, points // blocks, sources, modes // sources)
    extra = held_rows - modes // sources
    both = np.pad(both, ((0, 0), (0, 0), (0, 0), (0, 0), (0, extra)))
    both = np.transpose(both, (1, 0, 2, 3, 4))
    return jnp.asarray(both.reshape(blocks, 2 * (points // blocks), -1).astype(jnp.bfloat16))


def x_table(count, points, sources):
    cosine, sine = circle(np.arange(count), np.arange(points), points)
    factor = np.where(np.arange(count) == 0, 1.0, 2.0).astype(np.float32)[:, None]
    cosine, sine = (part.astype(jnp.bfloat16).astype(np.float32) for part in (cosine, sine))
    table = np.stack([factor * cosine, -(factor * sine)], 0)
    table = table.reshape(2, sources, count // sources, points)
    extra = padded(count // sources) - count // sources
    table = np.pad(table, ((0, 0), (0, 0), (0, extra), (0, 0)))
    return jnp.asarray(table.reshape(2, -1, points).astype(jnp.bfloat16))


def estimate(rows, depth, columns):
    return pl.CostEstimate(
        flops=2 * rows * depth * columns,
        bytes_accessed=2 * (rows * depth + depth * columns + rows * columns),
        transcendentals=0,
    )


MESH = pl.DeviceIdType.MESH
CHUNK = 8
SLOTS = 3


def grouping(kx, ky):
    if kx % 4 == 0 and ky % 4 == 0:
        return 4, ky
    return 1, padded(ky)


def pieces_of(kx):
    return [(start, min(CHUNK, kx - start)) for start in range(0, kx, CHUNK)]


def exchange(rows, cols, modes_ref, table_z, table_y, out_ref, modes, sent, came, ready, total, passed,
             in_sem, send_z, recv_z, send_y, recv_y):
    kx, ky = modes.shape[1], modes.shape[2]
    width = came.shape[3]
    half = width // 2
    y_local = out_ref.shape[2]
    at_col, at_row = lax.axis_index("col"), lax.axis_index("row")
    group, held = grouping(kx, ky)
    block = group * held
    pieces = pieces_of(kx)
    count = len(pieces)
    pair = ready.shape[2] // width

    def load(c):
        return pltpu.make_async_copy(modes_ref.at[c], modes.at[c], in_sem.at[c])

    for c in range(3):
        load(c).start()
    barrier = pltpu.get_barrier_semaphore()
    for r in range(1, cols):
        peer = lax.rem(at_col + r, cols)
        pl.semaphore_signal(barrier, inc=1, device_id={"col": peer}, device_id_type=MESH)
    for r in range(1, rows):
        peer = lax.rem(at_row + r, rows)
        pl.semaphore_signal(barrier, inc=1, device_id={"row": peer}, device_id_type=MESH)

    def z_copy(t, r, size):
        peer = lax.rem(at_col + r, cols)
        used = pl.ds(0, size * held)
        return pltpu.make_async_remote_copy(
            src_ref=sent.at[t, peer, used], dst_ref=came.at[t, at_col, used],
            send_sem=send_z.at[t, r], recv_sem=recv_z.at[t, r],
            device_id={"col": peer}, device_id_type=MESH)

    def y_copy(c, j, r):
        peer = lax.rem(at_row + r, rows)
        return pltpu.make_async_remote_copy(
            src_ref=passed.at[j % SLOTS, peer],
            dst_ref=out_ref.at[at_row, c, :, pl.ds(j * CHUNK, CHUNK), :],
            send_sem=send_y.at[c, j, r], recv_sem=recv_y.at[c, j, r],
            device_id={"row": peer}, device_id_type=MESH)

    def y_own(c, j):
        return pltpu.make_async_copy(
            passed.at[j % SLOTS, at_row],
            out_ref.at[at_row, c, :, pl.ds(j * CHUNK, CHUNK), :], send_y.at[c, j, 0])

    def y_left(c, j):
        y_own(c, j).wait()
        for r in range(1, rows):
            y_copy(c, j, r).wait_send()

    total[...] = jnp.zeros_like(total)

    @pl.loop(0, 3)
    def _(c):
        load(c).wait()
        for j, (start, size) in enumerate(pieces):
            t = c * count + j

            @pl.loop(0, size // group)
            def _(g):
                slabs = [modes[c, start + g * group + i] for i in range(group)]
                data = slabs[0] if group == 1 else jnp.concatenate(slabs, 0)
                value = jnp.dot(data, table_z[...], preferred_element_type=jnp.float32)
                value = value.astype(jnp.bfloat16)
                if value.shape[0] < block:
                    spare = jnp.zeros((block - value.shape[0], value.shape[1]), jnp.bfloat16)
                    value = jnp.concatenate([value, spare], 0)
                at = pl.ds(pl.multiple_of(g * block, 16), block)
                for b in range(cols):
                    sent[t, b, at, :] = value[:, b * width : (b + 1) * width]
                came[t, at_col, at, :] = sent[t, at_col, at, :]

            if j == 0:
                @pl.when(c == 0)
                def _():
                    pl.semaphore_wait(barrier, cols + rows - 2)
            for r in range(1, cols):
                z_copy(t, r, size).start()

    @pl.loop(0, 3)
    def _(c):
        for j, (start, size) in enumerate(pieces):
            t = c * count + j
            for r in range(1, cols):
                z_copy(t, r, size).wait_recv()

            @pl.loop(0, size // group)
            def _(g):
                at = pl.ds(pl.multiple_of(g * block, 16), block)
                blocks = [came[t, s, at, :] for s in range(cols)]
                lines = []
                for i in range(group):
                    parts = [part[i * held : (i + 1) * held] for part in blocks]
                    lines.append(jnp.concatenate(parts, 0))
                for i in range(0, group, pair):
                    line = lines[i] if pair == 1 else jnp.concatenate(lines[i : i + pair], 1)
                    ready[g * (group // pair) + i // pair] = line

            if j >= SLOTS:
                y_left(c, j - SLOTS)
            elif count - SLOTS + j >= 0:
                @pl.when(c > 0)
                def _():
                    y_left(c - 1, count - SLOTS + j)

            @pl.loop(0, rows)
            def _(q):
                r = lax.rem(q + rows // 2, rows)
                peer = lax.rem(at_row + r, rows)
                for a in range(0, size, pair):
                    product = jnp.dot(
                        table_y[peer], ready[a // pair], preferred_element_type=jnp.float32
                    )
                    for g in range(pair):
                        by_cos = product[:y_local, g * width : (g + 1) * width]
                        by_sin = product[y_local:, g * width : (g + 1) * width]
                        swap = jnp.concatenate([-by_sin[:, half:], by_sin[:, :half]], 1)
                        total[:, a + g, :] = by_cos + swap
                if size < CHUNK:
                    total[:, size:, :] = jnp.zeros((y_local, CHUNK - size, width), jnp.float32)
                passed[j % SLOTS, peer] = total[...].astype(jnp.bfloat16)

                @pl.when(r == 0)
                def _():
                    y_own(c, j).start()

                @pl.when(r != 0)
                def _():
                    y_copy(c, j, r).start()

    @pl.loop(0, 3)
    def _(c):
        for j, (start, size) in enumerate(pieces):
            for r in range(1, cols):
                z_copy(c * count + j, r, size).wait_send()
            for r in range(1, rows):
                y_copy(c, j, r).wait_recv()

    for j in range(max(count - SLOTS, 0), count):
        y_left(2, j)


def gather(rows, cols, by_cos, by_sin, cos_y, sin_y, out_ref, mine, wide, tall, sums,
           send_c, recv_c, send_r, recv_r):
    at_col, at_row = lax.axis_index("col"), lax.axis_index("row")
    barrier = pltpu.get_barrier_semaphore()
    for r in range(1, cols):
        peer = lax.rem(at_col + r, cols)
        pl.semaphore_signal(barrier, inc=1, device_id={"col": peer}, device_id_type=MESH)
    for r in range(1, rows):
        peer = lax.rem(at_row + r, rows)
        pl.semaphore_signal(barrier, inc=1, device_id={"row": peer}, device_id_type=MESH)

    def swapped(value):
        half = value.shape[1] // 2
        return jnp.concatenate([value[:, half:], -value[:, :half]], 1)

    both = by_cos[...] + swapped(by_sin[...])
    both = both * cos_y[...] + swapped(both) * sin_y[...]
    mine[...] = jnp.broadcast_to(jnp.sum(both, 0, keepdims=True), mine.shape)
    pl.semaphore_wait(barrier, cols + rows - 2)

    def col_copy(r):
        return pltpu.make_async_remote_copy(
            src_ref=mine, dst_ref=wide.at[r], send_sem=send_c.at[r], recv_sem=recv_c.at[r],
            device_id={"col": lax.rem(at_col + r, cols)}, device_id_type=MESH)

    def row_copy(r):
        return pltpu.make_async_remote_copy(
            src_ref=sums, dst_ref=tall.at[r], send_sem=send_r.at[r], recv_sem=recv_r.at[r],
            device_id={"row": lax.rem(at_row + r, rows)}, device_id_type=MESH)

    for r in range(1, cols):
        col_copy(r).start()
    result = mine[...]
    for r in range(1, cols):
        col_copy(r).wait_recv()
        result = result + wide[r]
    sums[...] = result
    for r in range(1, rows):
        row_copy(r).start()
    for r in range(1, rows):
        row_copy(r).wait_recv()
        result = result + tall[r]
    out_ref[...] = result
    for r in range(1, cols):
        col_copy(r).wait_send()
    for r in range(1, rows):
        row_copy(r).wait_send()


def along_x(arrived_0, arrived_1, arrived_2, table_ref, phase_ref, weight_ref, cos_ref, sin_ref,
            velocity_ref, by_cos_ref, by_sin_ref, real_scr, imag_scr):
    ys, width = arrived_0.shape[2], arrived_0.shape[4]
    half = width // 2
    fields = []
    for c, arrived_ref in enumerate((arrived_0, arrived_1, arrived_2)):
        for y in range(ys):
            data = arrived_ref[:, 0, y].reshape(-1, width).T
            real_scr[c, y * half : (y + 1) * half, :] = data[:half]
            imag_scr[c, y * half : (y + 1) * half, :] = data[half:]
        field = jnp.dot(real_scr[c], table_ref[0], preferred_element_type=jnp.float32)
        field = field + jnp.dot(imag_scr[c], table_ref[1], preferred_element_type=jnp.float32)
        velocity_ref[c] = field.astype(jnp.bfloat16).reshape(velocity_ref.shape[1:])
        fields.append(field)
    f0, f1, f2 = fields
    trace = (f0 * f0 + f1 * f1 + f2 * f2) / 3.0
    stress = [f0 * f0 - trace, f1 * f1 - trace, f2 * f2 - trace, f0 * f1, f0 * f2, f1 * f2]
    mixed = None
    for index, part in enumerate(stress):
        line = jnp.dot(
            part.astype(jnp.bfloat16), phase_ref[...], preferred_element_type=jnp.float32
        )
        term = weight_ref[index : index + 1, :] * line
        mixed = term if mixed is None else mixed + term
    mixed = mixed.reshape(ys, half, -1)
    by_cos_ref[...] = jnp.sum(mixed * cos_ref[...][None], 1)
    by_sin_ref[...] = jnp.sum(mixed * sin_ref[...][None], 1)


def body(rows, cols, velocity_modes, wavenumbers, polar, azimuth):
    kx_local, ky_local, modes = velocity_modes.shape[1:]
    modes = modes // 2
    kx = kx_local * rows
    points = velocity_points(modes)
    y_local, z_local = points // rows, points // cols
    width = 2 * z_local
    kx_pad = padded(kx_local)

    group, held = grouping(kx_local, ky_local)
    pair = 2 if group % 2 == 0 and width % 128 == 0 else 1
    count = len(pieces_of(kx_local))
    table_z = z_table(modes, points, cols)
    table_y = y_table(modes, points, cols, rows, held)
    arrived = pl.pallas_call(
        functools.partial(exchange, rows, cols),
        in_specs=[
            pl.BlockSpec(memory_space=pl.ANY),
            pl.BlockSpec(memory_space=pltpu.VMEM),
            pl.BlockSpec(memory_space=pltpu.VMEM),
        ],
        out_specs=pl.BlockSpec(memory_space=pl.ANY),
        out_shape=jax.ShapeDtypeStruct((rows, 3, y_local, kx_pad, width), jnp.bfloat16),
        scratch_shapes=[
            pltpu.VMEM(velocity_modes.shape, jnp.bfloat16),
            pltpu.VMEM((3 * count, cols, CHUNK * held, width), jnp.bfloat16),
            pltpu.VMEM((3 * count, cols, CHUNK * held, width), jnp.bfloat16),
            pltpu.VMEM((CHUNK // pair, cols * held, pair * width), jnp.bfloat16),
            pltpu.VMEM((y_local, CHUNK, width), jnp.float32),
            pltpu.VMEM((SLOTS, rows, y_local, CHUNK, width), jnp.bfloat16),
            pltpu.SemaphoreType.DMA((3,)),
            pltpu.SemaphoreType.DMA((3 * count, cols)),
            pltpu.SemaphoreType.DMA((3 * count, cols)),
            pltpu.SemaphoreType.DMA((3, count, rows)),
            pltpu.SemaphoreType.DMA((3, count, rows)),
        ],
        compiler_params=pltpu.CompilerParams(
            vmem_limit_bytes=VMEM_LIMIT, collective_id=0, has_side_effects=True
        ),
        cost_estimate=estimate(3 * 2 * points, cols * ky_local, 2 * kx_local * width),
        name="exchange",
    )(velocity_modes, table_z, table_y)

    dirs, freqs = polar.shape[0], wavenumbers.shape[0]
    count_j = dirs * freqs
    wave_j = jnp.repeat(wavenumbers, dirs)
    axis_one = jnp.tile(jnp.sin(polar) * jnp.cos(azimuth), freqs)
    axis_two = jnp.tile(jnp.sin(polar) * jnp.sin(azimuth), freqs)
    axis_three = jnp.tile(jnp.cos(polar), freqs)
    unit = 2.0 * math.pi / points
    x_pos = jnp.arange(points, dtype=jnp.int32).astype(jnp.float32) * unit
    angle_x = wave_j[None, :] * (axis_one[None, :] * x_pos[:, None])
    phase_x = jnp.concatenate([jnp.cos(angle_x), -jnp.sin(angle_x)], 1).astype(jnp.bfloat16)
    weights = jnp.stack(
        [
            axis_one * axis_one,
            axis_two * axis_two,
            axis_three * axis_three,
            2.0 * axis_one * axis_two,
            2.0 * axis_one * axis_three,
            2.0 * axis_two * axis_three,
        ],
        0,
    )
    weights = jnp.concatenate([weights, weights], 1)
    z_index = lax.axis_index("col") * z_local + jnp.arange(z_local, dtype=jnp.int32)
    y_index = lax.axis_index("row") * y_local + jnp.arange(y_local, dtype=jnp.int32)
    angle_z = wave_j[None, :] * (axis_three[None, :] * (z_index.astype(jnp.float32) * unit)[:, None])
    angle_y = wave_j[None, :] * (axis_two[None, :] * (y_index.astype(jnp.float32) * unit)[:, None])
    cos_z, sin_z = jnp.cos(angle_z), jnp.sin(angle_z)

    ys = 8
    whole = lambda i: (0, 0)
    velocity, by_cos, by_sin = pl.pallas_call(
        along_x,
        grid=(y_local // ys,),
        in_specs=[
            *[
                pl.BlockSpec((rows, 1, ys, kx_pad, width), lambda i, c=c: (0, c, i, 0, 0))
                for c in range(3)
            ],
            pl.BlockSpec((2, rows * kx_pad, points), lambda i: (0, 0, 0)),
            pl.BlockSpec((points, 2 * count_j), whole),
            pl.BlockSpec((6, 2 * count_j), whole),
            pl.BlockSpec((z_local, 2 * count_j), whole),
            pl.BlockSpec((z_local, 2 * count_j), whole),
        ],
        out_specs=[
            pl.BlockSpec((3, ys, z_local, points), lambda i: (0, i, 0, 0)),
            pl.BlockSpec((ys, 2 * count_j), lambda i: (i, 0)),
            pl.BlockSpec((ys, 2 * count_j), lambda i: (i, 0)),
        ],
        out_shape=[
            jax.ShapeDtypeStruct((3, y_local, z_local, points), jnp.bfloat16),
            jax.ShapeDtypeStruct((y_local, 2 * count_j), jnp.float32),
            jax.ShapeDtypeStruct((y_local, 2 * count_j), jnp.float32),
        ],
        scratch_shapes=[pltpu.VMEM((3, ys * z_local, rows * kx_pad), jnp.bfloat16)] * 2,
        compiler_params=pltpu.CompilerParams(vmem_limit_bytes=VMEM_LIMIT),
        name="along_x",
    )(
        arrived,
        arrived,
        arrived,
        x_table(kx, points, rows),
        phase_x,
        weights,
        jnp.concatenate([cos_z, cos_z], 1),
        jnp.concatenate([sin_z, sin_z], 1),
    )
    cos_y, sin_y = jnp.cos(angle_y), jnp.sin(angle_y)
    peers = lambda n: pltpu.SemaphoreType.DMA((n,))
    tile = (8, 2 * count_j)
    terms = pl.pallas_call(
        functools.partial(gather, rows, cols),
        in_specs=[pl.BlockSpec(memory_space=pltpu.VMEM)] * 4,
        out_specs=pl.BlockSpec(memory_space=pltpu.VMEM),
        out_shape=jax.ShapeDtypeStruct(tile, jnp.float32),
        scratch_shapes=[
            pltpu.VMEM(tile, jnp.float32),
            pltpu.VMEM((cols, *tile), jnp.float32),
            pltpu.VMEM((rows, *tile), jnp.float32),
            pltpu.VMEM(tile, jnp.float32),
            peers(cols), peers(cols), peers(rows), peers(rows),
        ],
        compiler_params=pltpu.CompilerParams(collective_id=1, has_side_effects=True),
        name="gather",
    )(by_cos, by_sin, jnp.concatenate([cos_y, cos_y], 1), jnp.concatenate([sin_y, sin_y], 1))
    spectrum = terms[0].reshape(2, freqs, dirs) * (wavenumbers * wavenumbers)[None, :, None]
    total = jnp.transpose(spectrum / points**1.5, (2, 0, 1))
    owned = dirs // cols
    far_field = lax.dynamic_slice_in_dim(total, lax.axis_index("col") * owned, owned, 0)
    return (velocity, far_field)


def velocity_points(modes):
    return 1 << (modes - 1).bit_length()


def solution(mesh):
    return jax.shard_map(
        functools.partial(body, mesh.shape["row"], mesh.shape["col"]),
        mesh=mesh,
        in_specs=(P(None, "row", "col", None), P(), P(), P()),
        out_specs=(P(None, "row", "col", None), P("col", None, None)),
        check_vma=False,
    )
```

time: 457 us -> 381 us (0.83)
  blocking collectives: 51.4 us -> 0 us
  other arithmetic: 18.1 us -> 6.03 us
  Pallas kernels: 381 us -> 371 us
    psum x1 -> x0, blocking collectives: 51.4 us -> none  [body(): total = lax.psum(spectrum, ('row', 'col'))]
    pallas_call x1, Pallas kernels: 340 us -> 311 us  [body(): pl.pallas_call(functools.partial(exchange, rows, cols), in_specs=[pl.Bloc...]
    pallas_call x0 -> x1, Pallas kernels: none -> 19.2 us  [body(): pl.pallas_call(functools.partial(gather, rows, cols), in_specs=[pl.BlockS...]
    another operation x5 -> x2, other arithmetic: 10 us -> 1.88 us
where the time goes in v2:
time: 381 us
  Pallas kernels  371 us (97%)
  other arithmetic  6.03 us (2%)
    pallas_call x1, Pallas kernels, body(): pl.pallas_call(functools.partial(exchange, rows, cols), in_specs=[pl.Bloc...  311 us
    pallas_call x1, Pallas kernels, body(): pl.pallas_call(along_x, grid=(y_local // ys,), in_specs=[*[pl.BlockSpec((...  40.9 us
    pallas_call x1, Pallas kernels, body(): pl.pallas_call(functools.partial(gather, rows, cols), in_specs=[pl.BlockS...  19.2 us

profile of v2, /device:TPU:0, one launch (start us, length us, event | category | flops | bytes accessed | tf_op | source)
XLA Modules:
  0.0 380.7 jit_solution(1871485860831151816)
XLA Ops:
  0.6 0.7 fusion.6
  1.3 0.7 broadcast_multiply_fusion
  2.0 0.1 tile.32
  2.1 0.1 mul.233
  2.2 0.1 tile.34
  2.3 0.1 mul.228
  2.4 0.7 pad_maximum_fusion.5.weight_ref
  3.1 0.1 mul.239
  3.2 0.7 broadcast_in_dim.2
  3.9 0.1 mul.217
  4.0 0.2 fusion.2
  4.2 0.7 pad_maximum_fusion.3
  4.9 0.1 mul.220
  5.0 1.2 cosine_convert_fusion
  6.2 0.8 pad_maximum_fusion.phase_ref
  6.9 310.9 %exchange.1.arrived_0.arrived_1.arrived_2 = bf16[4,3,128,48,128]{4,3,2,1,0:T(8,128)(2,1)} custom-call(bf16[3,44,44,704]{3,2,1,0:T(8,128)(2,1)} %modes_ref.1, bf16[704,1024]{1,0:T(8,128)(2,1)} %constant.31.clone.table_z, bf16[4,256,352]{2,1,0:T(8,128)(2,1)} %constant.32.clone.table_y), custom_call_target="tpu_custom_call" | custom-call | flops 24360517632 | bytes 79298560 | tf_op jit(solution)/shard_map/exchange/pallas_call | solution.py:313
  317.9 0.0 copy-start
  317.9 40.9 %along_x.1 = (bf16[3,128,64,512]{3,2,1,0:T(8,128)(2,1)}, f32[128,128]{1,0:T(8,128)}, f32[128,128]{1,0:T(8,128)}) custom-call(bf16[4,3,128,48,128]{4,3,2,1,0:T(8,128)(2,1)} %exchange.1.arrived_0.arrived_1.arrived_2, bf16[4,3,128,48,128]{4,3,2,1,0:T(8,128)(2,1)} %exchange.1.arrived_0.arrived_1.arrived_2, ...), custom_call_target="tpu_custom_call" | custom-call | tf_op jit(solution)/shard_map/along_x/pallas_call | solution.py:372
  358.8 0.1 mul.248
  358.9 0.3 fusion
  359.2 0.8 pad_maximum_fusion.1
  360.0 19.2 %gather.1 = f32[8,128]{1,0:T(8,128)} custom-call(f32[128,128]{1,0:T(8,128)} %get-tuple-element.6.by_cos, f32[128,128]{1,0:T(8,128)} %get-tuple-element.7.by_sin, f32[128,128]{1,0:T(8,128)} %get-tuple-element.26.cos_y, f32[128,128]{1,0:T(8,128)} %get-tuple-element.27.sin_y), custom_call_target="tpu_custom_call" | custom-call | tf_op jit(solution)/shard_map/gather/pallas_call | solution.py:412
  379.2 0.7 slice_reduce_fusion
  379.9 0.1 reshape_squeeze.3
  380.0 0.0 copy-done
  380.0 0.7 fusion.5
  (12 shorter events, 0.1 us)
Async XLA Ops:
  317.9 62.1 %copy-start = (f32[8]{0:T(128)S(1)}, f32[8]{0:T(128)}, u32[]{:S(2)}) copy-start(f32[8]{0:T(128)} %param.8) | copy-start | bytes 100

commit v3 on v2

v3 whole, which is shorter than its diff:
```python
import functools
import math

import jax
import jax.numpy as jnp
import numpy as np
from jax import lax
from jax.experimental import pallas as pl
from jax.experimental.pallas import tpu as pltpu
from jax.sharding import PartitionSpec as P

VMEM_LIMIT = 60 * 1024 * 1024


def padded(count):
    return -(-count // 16) * 16


def lanes(count):
    return -(-count // 128) * 128


def circle(waves, cells, points):
    angle = np.mod(np.outer(waves, cells), points).astype(np.float64) * (2.0 * math.pi / points)
    return np.cos(angle).astype(np.float32), np.sin(angle).astype(np.float32)


def z_table(modes, points, blocks):
    cosine, sine = circle(np.arange(modes) - modes // 2, np.arange(points), points)
    cosine, sine = (part.reshape(modes, blocks, 1, -1) for part in (cosine, sine))
    table = np.concatenate(
        [np.concatenate([cosine, sine], 2), np.concatenate([-sine, cosine], 2)], 0
    )
    return jnp.asarray(table.reshape(2 * modes, 2 * points).astype(jnp.bfloat16))


def estimate(rows, depth, columns):
    return pl.CostEstimate(
        flops=2 * rows * depth * columns,
        bytes_accessed=2 * (rows * depth + depth * columns + rows * columns),
        transcendentals=0,
    )


MESH = pl.DeviceIdType.MESH
CHUNK = 8
SLOTS = 3
WINDOW = 2


def grouping(kx, ky):
    if kx % 4 == 0 and ky % 4 == 0:
        return 4, ky
    return 1, padded(ky)


def pieces_of(kx):
    first = kx % CHUNK or CHUNK
    starts = [0, *range(first, kx, CHUNK)]
    return [(start, CHUNK if start else first) for start in starts]


def spread(ref, inner, shape):
    lane = lax.broadcasted_iota(jnp.int32, shape, 1)
    count = ref.shape[0]
    total = jnp.zeros(shape, jnp.float32)
    for start in range(0, shape[1], inner):
        here = jnp.logical_and(lane >= start, lane < start + inner)
        total = jnp.where(here, ref[(start // inner) % count], total)
    return total


def turn(waves, cells, points):
    product = jnp.bitwise_and(waves * cells, points - 1)
    return product.astype(jnp.float32) * (2.0 * math.pi / points)


def y_tables(table_y, held, ky):
    blocks, double, depth = table_y.shape
    cells = double // 2
    points = blocks * cells
    modes = depth // held * ky
    tile = min(cells, 64)

    @pl.loop(0, points // tile)
    def _(i):
        shape = (tile, depth)
        lane = lax.broadcasted_iota(jnp.int32, shape, 1)
        source = jnp.floor((lane.astype(jnp.float32) + 0.5) / held).astype(jnp.int32)
        slot = lane - source * held
        cell = lax.broadcasted_iota(jnp.int32, shape, 0) + i * tile
        angle = turn(source * ky + slot - modes // 2, cell, points)
        block = i // (cells // tile)
        at = pl.multiple_of(lax.rem(i, cells // tile) * tile, tile)
        for base, part in ((0, jnp.cos(angle)), (cells, jnp.sin(angle))):
            part = jnp.where(slot < ky, part, 0.0).astype(jnp.bfloat16)
            table_y[block, pl.ds(base + at, tile), :] = part


def x_tables(table_x, rows, kx):
    depth, points = table_x.shape[0] // 2, table_x.shape[1]
    held = padded(kx)
    first = pieces_of(kx)[0][1]
    table_x[...] = jnp.zeros_like(table_x)

    @pl.loop(0, rows)
    def _(source):
        shape = (held, points)
        slot = lax.broadcasted_iota(jnp.int32, shape, 0)
        local = jnp.where(slot < first, slot, slot - (CHUNK - first))
        keep = jnp.logical_and(
            jnp.logical_or(slot < first, slot >= CHUNK), local < kx
        )
        wave = source * kx + local
        angle = turn(wave, lax.broadcasted_iota(jnp.int32, shape, 1), points)
        factor = jnp.where(keep, jnp.where(wave == 0, 1.0, 2.0), 0.0)
        for base, part in ((0, jnp.cos(angle)), (depth, -jnp.sin(angle))):
            part = factor * part.astype(jnp.bfloat16).astype(jnp.float32)
            at = pl.ds(pl.multiple_of(base + source * held, 16), held)
            table_x[at, :] = part.astype(jnp.bfloat16)


def phases(wave_ref, polar_ref, azimuth_ref, phase_ref, weight_ref, z_ref, y_ref, at_col, at_row):
    points, count = phase_ref.shape
    dirs = polar_ref.shape[0]
    row = (1, count)
    wave = spread(wave_ref, dirs, row)
    polar, azimuth = spread(polar_ref, 1, row), spread(azimuth_ref, 1, row)
    one = jnp.sin(polar) * jnp.cos(azimuth)
    two = jnp.sin(polar) * jnp.sin(azimuth)
    three = jnp.cos(polar)
    unit = 2.0 * math.pi / points

    def angle(axis, first, shape):
        at = lax.broadcasted_iota(jnp.int32, shape, 0) + first
        return wave * (axis * (at.astype(jnp.float32) * unit))

    square = [one * one, two * two, three * three]
    weights = [
        (2.0 * square[0] - square[1] - square[2]) / 3.0,
        (2.0 * square[1] - square[0] - square[2]) / 3.0,
        2.0 * one * two,
        2.0 * one * three,
        2.0 * two * three,
    ]
    for index, weight in enumerate(weights):
        weight_ref[index : index + 1, :] = weight
    weight_ref[5:8, :] = jnp.zeros((3, count), jnp.float32)
    tile = min(points, 64)

    @pl.loop(0, points // tile)
    def _(i):
        shape = (tile, count)
        at = angle(one, i * tile, shape)
        real = lax.broadcasted_iota(jnp.int32, shape, 1) < count // 2
        phase = jnp.where(real, jnp.cos(at), -jnp.sin(at))
        phase_ref[pl.ds(pl.multiple_of(i * tile, tile), tile), :] = phase.astype(jnp.bfloat16)

    for ref, axis, where, scale in (
        (z_ref, three, at_col, 1.0),
        (y_ref, two, at_row, wave * wave / points**1.5),
    ):
        held = ref.shape[1]
        at = angle(axis, where * held, (held, count))
        ref[0] = jnp.cos(at) * scale
        ref[1] = jnp.sin(at) * scale


def exchange(rows, cols, modes_ref, table_z, wave_ref, polar_ref, azimuth_ref,
             out_ref, table_x, phase_ref, weight_ref, z_ref, y_ref, table_y, modes, sent, came, ready, total, passed,
             in_sem, send_z, recv_z, send_y, recv_y):
    kx, ky = modes.shape[1], modes.shape[2]
    width = came.shape[3]
    half = width // 2
    y_local = out_ref.shape[2]
    at_col, at_row = lax.axis_index("col"), lax.axis_index("row")
    group, held = grouping(kx, ky)
    block = group * held
    pieces = pieces_of(kx)
    count = len(pieces)
    pair = ready.shape[2] // width

    def load(c):
        return pltpu.make_async_copy(modes_ref.at[c], modes.at[c], in_sem.at[c])

    for c in range(3):
        load(c).start()
    barrier = pltpu.get_barrier_semaphore()
    for r in range(1, cols):
        peer = lax.rem(at_col + r, cols)
        pl.semaphore_signal(barrier, inc=1, device_id={"col": peer}, device_id_type=MESH)
    for r in range(1, rows):
        peer = lax.rem(at_row + r, rows)
        pl.semaphore_signal(barrier, inc=1, device_id={"row": peer}, device_id_type=MESH)

    def z_copy(c, j, r):
        t = c * count + j
        peer = lax.rem(at_col + r, cols)
        used = pl.ds(0, pieces[j][1] * held)
        return pltpu.make_async_remote_copy(
            src_ref=sent.at[j, peer, used], dst_ref=came.at[t, at_col, used],
            send_sem=send_z.at[t, r], recv_sem=recv_z.at[t, r],
            device_id={"col": peer}, device_id_type=MESH)

    def y_copy(c, j, r):
        peer = lax.rem(at_row + r, rows)
        return pltpu.make_async_remote_copy(
            src_ref=passed.at[j % SLOTS, peer],
            dst_ref=out_ref.at[at_row, c, :, pl.ds(j * CHUNK, CHUNK), :],
            send_sem=send_y.at[c, j, r], recv_sem=recv_y.at[c, j, r],
            device_id={"row": peer}, device_id_type=MESH)

    def y_own(c, j):
        return pltpu.make_async_copy(
            passed.at[j % SLOTS, at_row],
            out_ref.at[at_row, c, :, pl.ds(j * CHUNK, CHUNK), :], send_y.at[c, j, 0])

    def y_left(c, j):
        y_own(c, j).wait()
        for r in range(1, rows):
            y_copy(c, j, r).wait_send()

    def z_make(c, j):
        start, size = pieces[j]
        t = c * count + j
        if j == 0:
            load(c).wait()

        @pl.loop(0, size // group)
        def _(g):
            slabs = [modes[c, start + g * group + i] for i in range(group)]
            data = slabs[0] if group == 1 else jnp.concatenate(slabs, 0)
            value = jnp.dot(data, table_z[...], preferred_element_type=jnp.float32)
            value = value.astype(jnp.bfloat16)
            if value.shape[0] < block:
                spare = jnp.zeros((block - value.shape[0], value.shape[1]), jnp.bfloat16)
                value = jnp.concatenate([value, spare], 0)
            at = pl.ds(pl.multiple_of(g * block, 16), block)
            for b in range(cols):
                sent[j, b, at, :] = value[:, b * width : (b + 1) * width]
            came[t, at_col, at, :] = sent[j, at_col, at, :]

    def z_start(c, j):
        for r in range(1, cols):
            z_copy(c, j, r).start()

    def ahead(c, j):
        return (c, j) if j < count else ahead(c + 1, j - count)

    total[...] = jnp.zeros_like(total)
    for u in range(min(WINDOW, 3 * count)):
        c, j = ahead(0, u)
        z_make(c, j)
        if u == 0:
            pl.semaphore_wait(barrier, cols + rows - 2)
        z_start(c, j)
    y_tables(table_y, held, ky)
    x_tables(table_x, rows, kx)
    phases(wave_ref, polar_ref, azimuth_ref, phase_ref, weight_ref, z_ref, y_ref, at_col, at_row)

    @pl.loop(0, 3)
    def _(c):
        for j, (start, size) in enumerate(pieces):
            t = c * count + j
            c_next, j_next = ahead(c, j + WINDOW)
            later = j + WINDOW >= count

            def make():
                if later:
                    for r in range(1, cols):
                        z_copy(c_next - 1, j_next, r).wait_send()
                else:
                    @pl.when(c > 0)
                    def _():
                        for r in range(1, cols):
                            z_copy(c - 1, j_next, r).wait_send()
                z_make(c_next, j_next)

            if later:
                pl.when(c_next < 3)(make)
            else:
                make()
            for r in range(1, cols):
                z_copy(c, j, r).wait_recv()
            if later:
                pl.when(c_next < 3)(functools.partial(z_start, c_next, j_next))
            else:
                z_start(c_next, j_next)

            @pl.loop(0, size // group)
            def _(g):
                at = pl.ds(pl.multiple_of(g * block, 16), block)
                blocks = [came[t, s, at, :] for s in range(cols)]
                lines = []
                for i in range(group):
                    parts = [part[i * held : (i + 1) * held] for part in blocks]
                    lines.append(jnp.concatenate(parts, 0))
                for i in range(0, group, pair):
                    line = lines[i] if pair == 1 else jnp.concatenate(lines[i : i + pair], 1)
                    ready[g * (group // pair) + i // pair] = line

            if j >= SLOTS:
                y_left(c, j - SLOTS)
            elif count - SLOTS + j >= 0:
                @pl.when(c > 0)
                def _():
                    y_left(c - 1, count - SLOTS + j)

            @pl.loop(0, rows)
            def _(q):
                step = jnp.where(lax.rem(at_row, 2) == 0, q, rows - q)
                r = lax.rem(step + rows // 2, rows)
                peer = lax.rem(at_row + r, rows)
                for a in range(0, size, pair):
                    product = jnp.dot(
                        table_y[peer], ready[a // pair], preferred_element_type=jnp.float32
                    )
                    for g in range(pair):
                        by_cos = product[:y_local, g * width : (g + 1) * width]
                        by_sin = product[y_local:, g * width : (g + 1) * width]
                        swap = jnp.concatenate([-by_sin[:, half:], by_sin[:, :half]], 1)
                        total[:, a + g, :] = by_cos + swap
                if size < CHUNK:
                    total[:, size:, :] = jnp.zeros((y_local, CHUNK - size, width), jnp.float32)
                passed[j % SLOTS, peer] = total[...].astype(jnp.bfloat16)

                @pl.when(r == 0)
                def _():
                    y_own(c, j).start()

                @pl.when(r != 0)
                def _():
                    y_copy(c, j, r).start()

    @pl.loop(0, 3)
    def _(c):
        for j, (start, size) in enumerate(pieces):
            for r in range(1, rows):
                y_copy(c, j, r).wait_recv()

    for j in range(count):
        for r in range(1, cols):
            z_copy(2, j, r).wait_send()
    for j in range(max(count - SLOTS, 0), count):
        y_left(2, j)


def gather(rows, cols, freqs, by_cos, by_sin, y_ref, out_ref, mine, wide, tall, sums,
           send_c, recv_c, send_r, recv_r):
    at_col, at_row = lax.axis_index("col"), lax.axis_index("row")
    barrier = pltpu.get_barrier_semaphore()
    for r in range(1, cols):
        peer = lax.rem(at_col + r, cols)
        pl.semaphore_signal(barrier, inc=1, device_id={"col": peer}, device_id_type=MESH)
    for r in range(1, rows):
        peer = lax.rem(at_row + r, rows)
        pl.semaphore_signal(barrier, inc=1, device_id={"row": peer}, device_id_type=MESH)

    def swapped(value):
        half = value.shape[1] // 2
        return jnp.concatenate([value[:, half:], -value[:, :half]], 1)

    both = by_cos[...] + swapped(by_sin[...])
    both = both * y_ref[0] + swapped(both) * y_ref[1]
    mine[...] = jnp.broadcast_to(jnp.sum(both, 0, keepdims=True), mine.shape)
    pl.semaphore_wait(barrier, cols + rows - 2)

    def col_copy(r):
        return pltpu.make_async_remote_copy(
            src_ref=mine, dst_ref=wide.at[r], send_sem=send_c.at[r], recv_sem=recv_c.at[r],
            device_id={"col": lax.rem(at_col + r, cols)}, device_id_type=MESH)

    def row_copy(r):
        return pltpu.make_async_remote_copy(
            src_ref=sums, dst_ref=tall.at[r], send_sem=send_r.at[r], recv_sem=recv_r.at[r],
            device_id={"row": lax.rem(at_row + r, rows)}, device_id_type=MESH)

    for r in range(1, cols):
        col_copy(r).start()
    result = mine[...]
    for r in range(1, cols):
        col_copy(r).wait_recv()
        result = result + wide[r]
    sums[...] = result
    for r in range(1, rows):
        row_copy(r).start()
    for r in range(1, rows):
        row_copy(r).wait_recv()
        result = result + tall[r]
    count = result.shape[1]
    dirs = count // (2 * freqs)
    lane = lax.broadcasted_iota(jnp.int32, result.shape, 1)
    part = lax.broadcasted_iota(jnp.int32, result.shape, 0)
    result = jnp.where((lane >= count // 2) == (part == 1), result, 0.0)
    shape = (count // 2, freqs)
    place = lax.broadcasted_iota(jnp.int32, shape, 0)
    freq = lax.broadcasted_iota(jnp.int32, shape, 1)
    for own in range(out_ref.shape[0]):
        direction = at_col * out_ref.shape[0] + own
        pick = jnp.where(place == freq * dirs + direction, 1.0, 0.0)
        pick = jnp.concatenate([pick, pick], 0)
        out_ref[own] = jnp.dot(
            result, pick, precision=lax.Precision.HIGHEST, preferred_element_type=jnp.float32
        )[:2]
    for r in range(1, cols):
        col_copy(r).wait_send()
    for r in range(1, rows):
        row_copy(r).wait_send()


def along_x(arrived_0, arrived_1, arrived_2, table_ref, phase_ref, weight_ref, z_ref,
            velocity_ref, by_cos_ref, by_sin_ref, real_scr, imag_scr):
    ys, width = arrived_0.shape[2], arrived_0.shape[4]
    half = width // 2
    held = real_scr.shape[2]
    depth = table_ref.shape[0] // 2
    fields = []
    for c, arrived_ref in enumerate((arrived_0, arrived_1, arrived_2)):
        for y in range(ys):
            data = arrived_ref[:, 0, y].reshape(-1, width).T
            real_scr[c, y * half : (y + 1) * half, :] = data[:half]
            imag_scr[c, y * half : (y + 1) * half, :] = data[half:]
        field = jnp.dot(real_scr[c], table_ref[0:held], preferred_element_type=jnp.float32)
        field = field + jnp.dot(
            imag_scr[c], table_ref[depth : depth + held], preferred_element_type=jnp.float32
        )
        velocity_ref[c] = field.astype(jnp.bfloat16).reshape(velocity_ref.shape[1:])
        fields.append(field)
    f0, f1, f2 = fields
    last = f2 * f2
    stress = [f0 * f0 - last, f1 * f1 - last, f0 * f1, f0 * f2, f1 * f2]
    mixed = None
    for index, part in enumerate(stress):
        line = jnp.dot(
            part.astype(jnp.bfloat16), phase_ref[...], preferred_element_type=jnp.float32
        )
        term = weight_ref[index : index + 1, :] * line
        mixed = term if mixed is None else mixed + term
    mixed = mixed.reshape(ys, half, -1)
    by_cos_ref[...] = jnp.sum(mixed * z_ref[0][None], 1)
    by_sin_ref[...] = jnp.sum(mixed * z_ref[1][None], 1)


def body(rows, cols, velocity_modes, wavenumbers, polar, azimuth):
    kx_local, ky_local, modes = velocity_modes.shape[1:]
    modes = modes // 2
    points = velocity_points(modes)
    y_local, z_local = points // rows, points // cols
    width = 2 * z_local
    kx_pad = padded(kx_local)

    group, held = grouping(kx_local, ky_local)
    pair = 2 if group % 2 == 0 and width % 128 == 0 else 1
    count = len(pieces_of(kx_local))
    dirs, freqs = polar.shape[0], wavenumbers.shape[0]
    width_j = 2 * dirs * freqs
    depth = lanes(rows * kx_pad)
    table_z = z_table(modes, points, cols)
    arrived, table_x, phase, weights, near_z, near_y = pl.pallas_call(
        functools.partial(exchange, rows, cols),
        in_specs=[
            pl.BlockSpec(memory_space=pl.ANY),
            pl.BlockSpec(memory_space=pltpu.VMEM),
            *[pl.BlockSpec(memory_space=pltpu.SMEM)] * 3,
        ],
        out_specs=[
            pl.BlockSpec(memory_space=pl.ANY),
            *[pl.BlockSpec(memory_space=pltpu.VMEM)] * 5,
        ],
        out_shape=[
            jax.ShapeDtypeStruct((rows, 3, y_local, kx_pad, width), jnp.bfloat16),
            jax.ShapeDtypeStruct((2 * depth, points), jnp.bfloat16),
            jax.ShapeDtypeStruct((points, width_j), jnp.bfloat16),
            jax.ShapeDtypeStruct((8, width_j), jnp.float32),
            jax.ShapeDtypeStruct((2, z_local, width_j), jnp.float32),
            jax.ShapeDtypeStruct((2, y_local, width_j), jnp.float32),
        ],
        scratch_shapes=[
            pltpu.VMEM((rows, 2 * y_local, cols * held), jnp.bfloat16),
            pltpu.VMEM(velocity_modes.shape, jnp.bfloat16),
            pltpu.VMEM((count, cols, CHUNK * held, width), jnp.bfloat16),
            pltpu.VMEM((3 * count, cols, CHUNK * held, width), jnp.bfloat16),
            pltpu.VMEM((CHUNK // pair, cols * held, pair * width), jnp.bfloat16),
            pltpu.VMEM((y_local, CHUNK, width), jnp.float32),
            pltpu.VMEM((SLOTS, rows, y_local, CHUNK, width), jnp.bfloat16),
            pltpu.SemaphoreType.DMA((3,)),
            pltpu.SemaphoreType.DMA((3 * count, cols)),
            pltpu.SemaphoreType.DMA((3 * count, cols)),
            pltpu.SemaphoreType.DMA((3, count, rows)),
            pltpu.SemaphoreType.DMA((3, count, rows)),
        ],
        compiler_params=pltpu.CompilerParams(
            vmem_limit_bytes=VMEM_LIMIT, collective_id=0, has_side_effects=True
        ),
        cost_estimate=estimate(3 * 2 * points, cols * ky_local, 2 * kx_local * width),
        name="exchange",
    )(velocity_modes, table_z, wavenumbers, polar, azimuth)

    ys = 16
    whole = lambda i: (0, 0)
    velocity, by_cos, by_sin = pl.pallas_call(
        along_x,
        grid=(y_local // ys,),
        in_specs=[
            *[
                pl.BlockSpec((rows, 1, ys, kx_pad, width), lambda i, c=c: (0, c, i, 0, 0))
                for c in range(3)
            ],
            pl.BlockSpec((2 * depth, points), whole),
            pl.BlockSpec((points, width_j), whole),
            pl.BlockSpec((8, width_j), whole),
            pl.BlockSpec((2, z_local, width_j), lambda i: (0, 0, 0)),
        ],
        out_specs=[
            pl.BlockSpec((3, ys, z_local, points), lambda i: (0, i, 0, 0)),
            pl.BlockSpec((ys, width_j), lambda i: (i, 0)),
            pl.BlockSpec((ys, width_j), lambda i: (i, 0)),
        ],
        out_shape=[
            jax.ShapeDtypeStruct((3, y_local, z_local, points), jnp.bfloat16),
            jax.ShapeDtypeStruct((y_local, width_j), jnp.float32),
            jax.ShapeDtypeStruct((y_local, width_j), jnp.float32),
        ],
        scratch_shapes=[
            pltpu.VMEM((3, ys * z_local, rows * kx_pad), jnp.bfloat16),
            pltpu.VMEM((3, ys * z_local, rows * kx_pad), jnp.bfloat16),
        ],
        compiler_params=pltpu.CompilerParams(vmem_limit_bytes=VMEM_LIMIT),
        name="along_x",
    )(
        arrived,
        arrived,
        arrived,
        table_x,
        phase,
        weights,
        near_z,
    )
    peers = lambda n: pltpu.SemaphoreType.DMA((n,))
    tile = (8, width_j)
    far_field = pl.pallas_call(
        functools.partial(gather, rows, cols, freqs),
        in_specs=[pl.BlockSpec(memory_space=pltpu.VMEM)] * 3,
        out_specs=pl.BlockSpec(memory_space=pltpu.VMEM),
        out_shape=jax.ShapeDtypeStruct((dirs // cols, 2, freqs), jnp.float32),
        scratch_shapes=[
            pltpu.VMEM(tile, jnp.float32),
            pltpu.VMEM((cols, *tile), jnp.float32),
            pltpu.VMEM((rows, *tile), jnp.float32),
            pltpu.VMEM(tile, jnp.float32),
            peers(cols), peers(cols), peers(rows), peers(rows),
        ],
        compiler_params=pltpu.CompilerParams(collective_id=1, has_side_effects=True),
        name="gather",
    )(by_cos, by_sin, near_y)
    return (velocity, far_field)


def velocity_points(modes):
    return 1 << (modes - 1).bit_length()


def solution(mesh):
    return jax.shard_map(
        functools.partial(body, mesh.shape["row"], mesh.shape["col"]),
        mesh=mesh,
        in_specs=(P(None, "row", "col", None), P(), P(), P()),
        out_specs=(P(None, "row", "col", None), P("col", None, None)),
        check_vma=False,
    )
```

time: 381 us -> 346 us (0.908)
  Pallas kernels: 371 us -> 343 us
  other arithmetic: 6.03 us -> 0 us
    pallas_call x1, Pallas kernels: 311 us -> 281 us  [body(): pl.pallas_call(functools.partial(exchange, rows, cols), in_specs=[pl.Bloc...]
    pallas_call x1, Pallas kernels: 19.2 us -> 29 us  [body(): pl.pallas_call(functools.partial(gather, rows, cols, freqs), in_specs=[pl...]
    pallas_call x1, Pallas kernels: 40.9 us -> 33.7 us  [body(): pl.pallas_call(along_x, grid=(y_local // ys,), in_specs=[*[pl.BlockSpec((...]
where the time goes in v3:
time: 346 us; the launch traced here: 345 us
  Pallas kernels  343 us (99%)
    pallas_call x1, Pallas kernels, body(): pl.pallas_call(functools.partial(exchange, rows, cols), in_specs=[pl.Bloc...  281 us
    pallas_call x1, Pallas kernels, body(): pl.pallas_call(along_x, grid=(y_local // ys,), in_specs=[*[pl.BlockSpec((...  33.7 us
    pallas_call x1, Pallas kernels, body(): pl.pallas_call(functools.partial(gather, rows, cols, freqs), in_specs=[pl...  29 us

profile of v3, /device:TPU:0, one launch (start us, length us, event | category | flops | bytes accessed | tf_op | source)
XLA Modules:
  0.0 345.3 jit_solution(7605015786352281605)
XLA Ops:
  0.6 280.7 %exchange.1 = (bf16[4,3,128,48,128]{4,3,2,1,0:T(8,128)(2,1)}, bf16[512,512]{1,0:T(8,128)(2,1)}, bf16[512,128]{1,0:T(8,128)(2,1)}, f32[8,128]{1,0:T(8,128)}, f32[...) custom-call(bf16[3,44,44,704]{3,2,1,0:T(8,128)(2,1)} %modes_ref.1, bf16[704,1024]{1,0:T(8,128)(2,1)} %constant.2.clone.table_z, ...), custom_call_target="tpu_custom_call" | custom-call | flops 24360517632 | bytes 79298560 | tf_op jit(solution)/shard_map/exchange/pallas_call | solution.py:459
  281.4 33.7 %along_x.1 = (bf16[3,128,64,512]{3,2,1,0:T(8,128)(2,1)}, f32[128,128]{1,0:T(8,128)}, f32[128,128]{1,0:T(8,128)}) custom-call(bf16[4,3,128,48,128]{4,3,2,1,0:T(8,128)(2,1)} %get-tuple-element.11.arrived_0.arrived_1.arrived_2, bf16[4,3,128,48,128]{4,3,2,1,0:T(8,128)(2,1)} %get-tuple-element.11.arrived_0.arrived_1.arrived_2, ...), custom_call_target="tpu_custom_call" | custom-call | tf_op jit(solution)/shard_map/along_x/pallas_call | solution.py:501
  315.1 29.0 %gather.1 = f32[1,2,8]{2,1,0:T(2,128)} custom-call(f32[128,128]{1,0:T(8,128)} %get-tuple-element.17.by_cos, f32[128,128]{1,0:T(8,128)} %get-tuple-element.18.by_sin, f32[2,128,128]{2,1,0:T(8,128)} %get-tuple-element.19.y_ref), custom_call_target="tpu_custom_call" | custom-call | tf_op jit(solution)/shard_map/gather/pallas_call | solution.py:541
  344.1 1.2 copy.8

commit v4 on v3

--- a/solution.py
+++ b/solution.py
@@ -136,16 +136,18 @@
         return wave * (axis * (at.astype(jnp.float32) * unit))
 
     square = [one * one, two * two, three * three]
+    trace = (square[0] + square[1] + square[2]) / 3.0
     weights = [
-        (2.0 * square[0] - square[1] - square[2]) / 3.0,
-        (2.0 * square[1] - square[0] - square[2]) / 3.0,
+        square[0] - trace,
+        square[1] - trace,
         2.0 * one * two,
+        square[2] - trace,
         2.0 * one * three,
         2.0 * two * three,
     ]
     for index, weight in enumerate(weights):
         weight_ref[index : index + 1, :] = weight
-    weight_ref[5:8, :] = jnp.zeros((3, count), jnp.float32)
+    weight_ref[6:8, :] = jnp.zeros((2, count), jnp.float32)
     tile = min(points, 64)
 
     @pl.loop(0, points // tile)
@@ -166,8 +168,29 @@
         ref[1] = jnp.sin(at) * scale
 
 
+def x_field(real, imag, table_ref):
+    held, depth = real.shape[1], table_ref.shape[0] // 2
+    field = jnp.dot(real, table_ref[0:held], preferred_element_type=jnp.float32)
+    return field + jnp.dot(
+        imag, table_ref[depth : depth + held], preferred_element_type=jnp.float32
+    )
+
+
+def x_lines(stress, first, phase_ref, weight_ref, z_ref, ys):
+    mixed = None
+    for index, part in enumerate(stress):
+        line = jnp.dot(
+            part.astype(jnp.bfloat16), phase_ref[...], preferred_element_type=jnp.float32
+        )
+        term = weight_ref[first + index : first + index + 1, :] * line
+        mixed = term if mixed is None else mixed + term
+    mixed = mixed.reshape(ys, -1, mixed.shape[1])
+    return jnp.sum(mixed * z_ref[0][None], 1), jnp.sum(mixed * z_ref[1][None], 1)
+
+
 def exchange(rows, cols, modes_ref, table_z, wave_ref, polar_ref, azimuth_ref,
-             out_ref, table_x, phase_ref, weight_ref, z_ref, y_ref, table_y, modes, sent, came, ready, total, passed,
+             out_ref, early_ref, early_cos, early_sin, table_x, phase_ref, weight_ref, z_ref, y_ref,
+             x_in, x_real, x_imag, x_out, in_x, out_x, table_y, modes, sent, came, ready, total, passed,
              in_sem, send_z, recv_z, send_y, recv_y):
     kx, ky = modes.shape[1], modes.shape[2]
     width = came.shape[3]
@@ -179,6 +202,79 @@
     pieces = pieces_of(kx)
     count = len(pieces)
     pair = ready.shape[2] // width
+    slots = passed.shape[0]
+    ys = x_in.shape[3]
+    y_blocks = y_local // ys
+
+    def x_load(b, e):
+        slot = lax.rem(b, 2)
+        at = pl.ds(pl.multiple_of(b * ys, ys), ys)
+        return pltpu.make_async_copy(
+            out_ref.at[:, e, at], x_in.at[slot, e], in_x.at[slot, e])
+
+    def x_store(b, e):
+        slot = lax.rem(b, 2)
+        at = pl.ds(pl.multiple_of(b * ys, ys), ys)
+        return pltpu.make_async_copy(
+            x_out.at[slot, e], early_ref.at[e, at], out_x.at[slot, e])
+
+    def x_run(low, high):
+        for e in range(2):
+            x_load(low, e).start()
+
+        @pl.loop(low, high)
+        def _(b):
+            slot = lax.rem(b, 2)
+
+            @pl.when(b + 1 < high)
+            def _():
+                for e in range(2):
+                    x_load(b + 1, e).start()
+
+            for e in range(2):
+                x_load(b, e).wait()
+
+            @pl.when(b >= low + 2)
+            def _():
+                for e in range(2):
+                    x_store(b - 2, e).wait()
+
+            fields = []
+            for e in range(2):
+                for y in range(ys):
+                    data = x_in[slot, e, :, y].reshape(-1, width).T
+                    x_real[e, y * half : (y + 1) * half, :] = data[:half]
+                    x_imag[e, y * half : (y + 1) * half, :] = data[half:]
+                field = x_field(x_real[e], x_imag[e], table_x)
+                x_out[slot, e] = field.astype(jnp.bfloat16).reshape(x_out.shape[2:])
+                fields.append(field)
+            for e in range(2):
+                x_store(b, e).start()
+            f0, f1 = fields
+            at = pl.ds(pl.multiple_of(b * ys, ys), ys)
+            early_cos[at, :], early_sin[at, :] = x_lines(
+                [f0 * f0, f1 * f1, f0 * f1], 0, phase_ref, weight_ref, z_ref, ys
+            )
+
+        for b in range(max(low, high - 2), high):
+            for e in range(2):
+                x_store(b, e).wait()
+
+    middle = count // 2
+    if middle < slots - 1 or middle >= count - 1 or y_blocks % 2:
+        middle = None
+    share = y_blocks // 2 if middle is not None else 0
+
+    def x_early(j):
+        if j == (count - 1 if middle is None else middle):
+            for c in range(2):
+                for i in range(count):
+                    for r in range(1, rows):
+                        y_copy(c, i, r).wait_recv()
+        if j == middle:
+            x_run(0, share)
+        if j == count - 1:
+            x_run(share, y_blocks)
 
     def load(c):
         return pltpu.make_async_copy(modes_ref.at[c], modes.at[c], in_sem.at[c])
@@ -205,14 +301,14 @@
     def y_copy(c, j, r):
         peer = lax.rem(at_row + r, rows)
         return pltpu.make_async_remote_copy(
-            src_ref=passed.at[j % SLOTS, peer],
+            src_ref=passed.at[j % slots, peer],
             dst_ref=out_ref.at[at_row, c, :, pl.ds(j * CHUNK, CHUNK), :],
             send_sem=send_y.at[c, j, r], recv_sem=recv_y.at[c, j, r],
             device_id={"row": peer}, device_id_type=MESH)
 
     def y_own(c, j):
         return pltpu.make_async_copy(
-            passed.at[j % SLOTS, at_row],
+            passed.at[j % slots, at_row],
             out_ref.at[at_row, c, :, pl.ds(j * CHUNK, CHUNK), :], send_y.at[c, j, 0])
 
     def y_left(c, j):
@@ -241,8 +337,12 @@
             came[t, at_col, at, :] = sent[j, at_col, at, :]
 
     def z_start(c, j):
-        for r in range(1, cols):
-            z_copy(c, j, r).start()
+        for i in reversed(range(cols - 1)):
+            low, high = cols - 1 - i, i
+            low = jnp.where(low <= at_col, low - 1, low)
+            high = jnp.where(high >= at_col, high + 1, high)
+            peer = jnp.where(at_col < cols // 2, low, high)
+            z_copy(c, j, lax.rem(peer - at_col + cols, cols)).start()
 
     def ahead(c, j):
         return (c, j) if j < count else ahead(c + 1, j - count)
@@ -299,12 +399,12 @@
                     line = lines[i] if pair == 1 else jnp.concatenate(lines[i : i + pair], 1)
                     ready[g * (group // pair) + i // pair] = line
 
-            if j >= SLOTS:
-                y_left(c, j - SLOTS)
-            elif count - SLOTS + j >= 0:
+            if j >= slots:
+                y_left(c, j - slots)
+            elif count - slots + j >= 0:
                 @pl.when(c > 0)
                 def _():
-                    y_left(c - 1, count - SLOTS + j)
+                    y_left(c - 1, count - slots + j)
 
             @pl.loop(0, rows)
             def _(q):
@@ -322,7 +422,7 @@
                         total[:, a + g, :] = by_cos + swap
                 if size < CHUNK:
                     total[:, size:, :] = jnp.zeros((y_local, CHUNK - size, width), jnp.float32)
-                passed[j % SLOTS, peer] = total[...].astype(jnp.bfloat16)
+                passed[j % slots, peer] = total[...].astype(jnp.bfloat16)
 
                 @pl.when(r == 0)
                 def _():
@@ -332,16 +432,17 @@
                 def _():
                     y_copy(c, j, r).start()
 
-    @pl.loop(0, 3)
-    def _(c):
-        for j, (start, size) in enumerate(pieces):
-            for r in range(1, rows):
-                y_copy(c, j, r).wait_recv()
+            if j == middle or j == count - 1:
+                pl.when(c == 2)(functools.partial(x_early, j))
+
+    for j in range(count):
+        for r in range(1, rows):
+            y_copy(2, j, r).wait_recv()
 
     for j in range(count):
         for r in range(1, cols):
             z_copy(2, j, r).wait_send()
-    for j in range(max(count - SLOTS, 0), count):
+    for j in range(max(count - slots, 0), count):
         y_left(2, j)
 
 
@@ -408,37 +509,25 @@
         row_copy(r).wait_send()
 
 
-def along_x(arrived_0, arrived_1, arrived_2, table_ref, phase_ref, weight_ref, z_ref,
+def along_x(arrived_ref, early_ref, early_cos, early_sin, table_ref, phase_ref, weight_ref, z_ref,
             velocity_ref, by_cos_ref, by_sin_ref, real_scr, imag_scr):
-    ys, width = arrived_0.shape[2], arrived_0.shape[4]
+    ys, width = arrived_ref.shape[2], arrived_ref.shape[4]
     half = width // 2
-    held = real_scr.shape[2]
-    depth = table_ref.shape[0] // 2
-    fields = []
-    for c, arrived_ref in enumerate((arrived_0, arrived_1, arrived_2)):
-        for y in range(ys):
-            data = arrived_ref[:, 0, y].reshape(-1, width).T
-            real_scr[c, y * half : (y + 1) * half, :] = data[:half]
-            imag_scr[c, y * half : (y + 1) * half, :] = data[half:]
-        field = jnp.dot(real_scr[c], table_ref[0:held], preferred_element_type=jnp.float32)
-        field = field + jnp.dot(
-            imag_scr[c], table_ref[depth : depth + held], preferred_element_type=jnp.float32
-        )
-        velocity_ref[c] = field.astype(jnp.bfloat16).reshape(velocity_ref.shape[1:])
-        fields.append(field)
-    f0, f1, f2 = fields
-    last = f2 * f2
-    stress = [f0 * f0 - last, f1 * f1 - last, f0 * f1, f0 * f2, f1 * f2]
-    mixed = None
-    for index, part in enumerate(stress):
-        line = jnp.dot(
-            part.astype(jnp.bfloat16), phase_ref[...], preferred_element_type=jnp.float32
-        )
-        term = weight_ref[index : index + 1, :] * line
-        mixed = term if mixed is None else mixed + term
-    mixed = mixed.reshape(ys, half, -1)
-    by_cos_ref[...] = jnp.sum(mixed * z_ref[0][None], 1)
-    by_sin_ref[...] = jnp.sum(mixed * z_ref[1][None], 1)
+    for y in range(ys):
+        data = arrived_ref[:, 0, y].reshape(-1, width).T
+        real_scr[y * half : (y + 1) * half, :] = data[:half]
+        imag_scr[y * half : (y + 1) * half, :] = data[half:]
+    f2 = x_field(real_scr[...], imag_scr[...], table_ref)
+    velocity_ref[2] = f2.astype(jnp.bfloat16).reshape(velocity_ref.shape[1:])
+    velocity_ref[0] = early_ref[0]
+    velocity_ref[1] = early_ref[1]
+    f0 = early_ref[0].reshape(ys * half, -1).astype(jnp.float32)
+    f1 = early_ref[1].reshape(ys * half, -1).astype(jnp.float32)
+    by_cos, by_sin = x_lines(
+        [f2 * f2, f0 * f2, f1 * f2], 3, phase_ref, weight_ref, z_ref, ys
+    )
+    by_cos_ref[...] = early_cos[...] + by_cos
+    by_sin_ref[...] = early_sin[...] + by_sin
 
 
 def body(rows, cols, velocity_modes, wavenumbers, polar, azimuth):
@@ -456,7 +545,7 @@
     width_j = 2 * dirs * freqs
     depth = lanes(rows * kx_pad)
     table_z = z_table(modes, points, cols)
-    arrived, table_x, phase, weights, near_z, near_y = pl.pallas_call(
+    arrived, early, early_cos, early_sin, table_x, phase, weights, near_z, near_y = pl.pallas_call(
         functools.partial(exchange, rows, cols),
         in_specs=[
             pl.BlockSpec(memory_space=pl.ANY),
@@ -465,10 +554,14 @@
         ],
         out_specs=[
             pl.BlockSpec(memory_space=pl.ANY),
-            *[pl.BlockSpec(memory_space=pltpu.VMEM)] * 5,
+            pl.BlockSpec(memory_space=pl.ANY),
+            *[pl.BlockSpec(memory_space=pltpu.VMEM)] * 7,
         ],
         out_shape=[
             jax.ShapeDtypeStruct((rows, 3, y_local, kx_pad, width), jnp.bfloat16),
+            jax.ShapeDtypeStruct((2, y_local, z_local, points), jnp.bfloat16),
+            jax.ShapeDtypeStruct((y_local, width_j), jnp.float32),
+            jax.ShapeDtypeStruct((y_local, width_j), jnp.float32),
             jax.ShapeDtypeStruct((2 * depth, points), jnp.bfloat16),
             jax.ShapeDtypeStruct((points, width_j), jnp.bfloat16),
             jax.ShapeDtypeStruct((8, width_j), jnp.float32),
@@ -476,13 +569,19 @@
             jax.ShapeDtypeStruct((2, y_local, width_j), jnp.float32),
         ],
         scratch_shapes=[
+            pltpu.VMEM((2, 2, rows, 8, kx_pad, width), jnp.bfloat16),
+            pltpu.VMEM((2, 8 * z_local, rows * kx_pad), jnp.bfloat16),
+            pltpu.VMEM((2, 8 * z_local, rows * kx_pad), jnp.bfloat16),
+            pltpu.VMEM((2, 2, 8, z_local, points), jnp.bfloat16),
+            pltpu.SemaphoreType.DMA((2, 2)),
+            pltpu.SemaphoreType.DMA((2, 2)),
             pltpu.VMEM((rows, 2 * y_local, cols * held), jnp.bfloat16),
             pltpu.VMEM(velocity_modes.shape, jnp.bfloat16),
             pltpu.VMEM((count, cols, CHUNK * held, width), jnp.bfloat16),
             pltpu.VMEM((3 * count, cols, CHUNK * held, width), jnp.bfloat16),
             pltpu.VMEM((CHUNK // pair, cols * held, pair * width), jnp.bfloat16),
             pltpu.VMEM((y_local, CHUNK, width), jnp.float32),
-            pltpu.VMEM((SLOTS, rows, y_local, CHUNK, width), jnp.bfloat16),
+            pltpu.VMEM((min(SLOTS, count), rows, y_local, CHUNK, width), jnp.bfloat16),
             pltpu.SemaphoreType.DMA((3,)),
             pltpu.SemaphoreType.DMA((3 * count, cols)),
             pltpu.SemaphoreType.DMA((3 * count, cols)),
@@ -502,10 +601,10 @@
         along_x,
         grid=(y_local // ys,),
         in_specs=[
-            *[
-                pl.BlockSpec((rows, 1, ys, kx_pad, width), lambda i, c=c: (0, c, i, 0, 0))
-                for c in range(3)
-            ],
+            pl.BlockSpec((rows, 1, ys, kx_pad, width), lambda i: (0, 2, i, 0, 0)),
+            pl.BlockSpec((2, ys, z_local, points), lambda i: (0, i, 0, 0)),
+            pl.BlockSpec((ys, width_j), lambda i: (i, 0)),
+            pl.BlockSpec((ys, width_j), lambda i: (i, 0)),
             pl.BlockSpec((2 * depth, points), whole),
             pl.BlockSpec((points, width_j), whole),
             pl.BlockSpec((8, width_j), whole),
@@ -522,15 +621,16 @@
             jax.ShapeDtypeStruct((y_local, width_j), jnp.float32),
         ],
         scratch_shapes=[
-            pltpu.VMEM((3, ys * z_local, rows * kx_pad), jnp.bfloat16),
-            pltpu.VMEM((3, ys * z_local, rows * kx_pad), jnp.bfloat16),
+            pltpu.VMEM((ys * z_local, rows * kx_pad), jnp.bfloat16),
+            pltpu.VMEM((ys * z_local, rows * kx_pad), jnp.bfloat16),
         ],
         compiler_params=pltpu.CompilerParams(vmem_limit_bytes=VMEM_LIMIT),
         name="along_x",
     )(
         arrived,
-        arrived,
-        arrived,
+        early,
+        early_cos,
+        early_sin,
         table_x,
         phase,
         weights,

time: 346 us -> 322 us (0.931)
  Pallas kernels: 343 us -> 319 us
    pallas_call x1, Pallas kernels: 29 us -> 11.4 us  [body(): pl.pallas_call(functools.partial(gather, rows, cols, freqs), in_specs=[pl...]
    pallas_call x1, Pallas kernels: 33.7 us -> 23 us  [body(): pl.pallas_call(along_x, grid=(y_local // ys,), in_specs=[pl.BlockSpec((ro...]
    pallas_call x1, Pallas kernels: 281 us -> 285 us  [body(): pl.pallas_call(functools.partial(exchange, rows, cols), in_specs=[pl.Bloc...]
where the time goes in v4:
time: 322 us; the launch traced here: 321 us
  Pallas kernels  319 us (99%)
    pallas_call x1, Pallas kernels, body(): pl.pallas_call(functools.partial(exchange, rows, cols), in_specs=[pl.Bloc...  285 us
    pallas_call x1, Pallas kernels, body(): pl.pallas_call(along_x, grid=(y_local // ys,), in_specs=[pl.BlockSpec((ro...  23 us
    pallas_call x1, Pallas kernels, body(): pl.pallas_call(functools.partial(gather, rows, cols, freqs), in_specs=[pl...  11.4 us

profile of v4, /device:TPU:0, one launch (start us, length us, event | category | flops | bytes accessed | tf_op | source)
XLA Modules:
  0.0 321.1 jit_solution(926044628992048520)
XLA Ops:
  0.6 284.8 %exchange.1 = (bf16[4,3,128,48,128]{4,3,2,1,0:T(8,128)(2,1)}, bf16[2,128,64,512]{3,2,1,0:T(8,128)(2,1)}, f32[128,128]{1,0:T(8,128)}, f32[128,128]{1,0:T(8,128)},...) custom-call(bf16[3,44,44,704]{3,2,1,0:T(8,128)(2,1)} %modes_ref.1, ...), custom_call_target="tpu_custom_call" | custom-call | flops 24360517632 | bytes 79298560 | tf_op jit(solution)/shard_map/exchange/pallas_call | solution.py:548
  285.4 23.0 %along_x.1 = (bf16[3,128,64,512]{3,2,1,0:T(8,128)(2,1)}, f32[128,128]{1,0:T(8,128)}, f32[128,128]{1,0:T(8,128)}) custom-call(bf16[4,3,128,48,128]{4,3,2,1,0:T(8,128)(2,1)} %get-tuple-element.14.arrived_ref, bf16[2,128,64,512]{3,2,1,0:T(8,128)(2,1)} %get-tuple-element.15.early_ref, f32[128,128]{1,0:T(8,128)} %get-tuple-element.16.early_cos, ...), custom_call_target="tpu_custom_call" | custom-call | tf_op jit(solution)/shard_map/along_x/pallas_call | solution.py:600
  308.4 11.4 %gather.1 = f32[1,2,8]{2,1,0:T(2,128)} custom-call(f32[128,128]{1,0:T(8,128)} %get-tuple-element.23.by_cos, f32[128,128]{1,0:T(8,128)} %get-tuple-element.24.by_sin, f32[2,128,128]{2,1,0:T(8,128)} %get-tuple-element.25.y_ref), custom_call_target="tpu_custom_call" | custom-call | tf_op jit(solution)/shard_map/gather/pallas_call | solution.py:641
  319.8 1.2 copy.8

commit v5 on v4

--- a/solution.py
+++ b/solution.py
@@ -263,7 +263,7 @@
     middle = count // 2
     if middle < slots - 1 or middle >= count - 1 or y_blocks % 2:
         middle = None
-    share = y_blocks // 2 if middle is not None else 0
+    share = y_blocks * 5 // 8 if middle is not None else 0
 
     def x_early(j):
         if j == (count - 1 if middle is None else middle):

time: 322 us -> 324 us (level)
  no operation moved by 1% of the time
where the time goes in v5:
time: 324 us; the launch traced here: 323 us
  Pallas kernels  322 us (99%)
    pallas_call x1, Pallas kernels, body(): pl.pallas_call(functools.partial(exchange, rows, cols), in_specs=[pl.Bloc...  287 us
    pallas_call x1, Pallas kernels, body(): pl.pallas_call(along_x, grid=(y_local // ys,), in_specs=[pl.BlockSpec((ro...  22.9 us
    pallas_call x1, Pallas kernels, body(): pl.pallas_call(functools.partial(gather, rows, cols, freqs), in_specs=[pl...  11.4 us

profile of v5, /device:TPU:0, one launch (start us, length us, event | category | flops | bytes accessed | tf_op | source)
XLA Modules:
  0.0 323.4 jit_solution(2638124063997904746)
XLA Ops:
  0.6 287.1 %exchange.1 = (bf16[4,3,128,48,128]{4,3,2,1,0:T(8,128)(2,1)}, bf16[2,128,64,512]{3,2,1,0:T(8,128)(2,1)}, f32[128,128]{1,0:T(8,128)}, f32[128,128]{1,0:T(8,128)},...) custom-call(bf16[3,44,44,704]{3,2,1,0:T(8,128)(2,1)} %modes_ref.1, ...), custom_call_target="tpu_custom_call" | custom-call | flops 24360517632 | bytes 79298560 | tf_op jit(solution)/shard_map/exchange/pallas_call | solution.py:548
  287.8 22.9 %along_x.1 = (bf16[3,128,64,512]{3,2,1,0:T(8,128)(2,1)}, f32[128,128]{1,0:T(8,128)}, f32[128,128]{1,0:T(8,128)}) custom-call(bf16[4,3,128,48,128]{4,3,2,1,0:T(8,128)(2,1)} %get-tuple-element.14.arrived_ref, bf16[2,128,64,512]{3,2,1,0:T(8,128)(2,1)} %get-tuple-element.15.early_ref, f32[128,128]{1,0:T(8,128)} %get-tuple-element.16.early_cos, ...), custom_call_target="tpu_custom_call" | custom-call | tf_op jit(solution)/shard_map/along_x/pallas_call | solution.py:600
  310.7 11.4 %gather.1 = f32[1,2,8]{2,1,0:T(2,128)} custom-call(f32[128,128]{1,0:T(8,128)} %get-tuple-element.23.by_cos, f32[128,128]{1,0:T(8,128)} %get-tuple-element.24.by_sin, f32[2,128,128]{2,1,0:T(8,128)} %get-tuple-element.25.y_ref), custom_call_target="tpu_custom_call" | custom-call | tf_op jit(solution)/shard_map/gather/pallas_call | solution.py:641
  322.2 1.2 copy.8
